TPU v7x, 8 devices: a whole 2x2x1 slice. The times are simulated.
8 devices in a mesh: dp: 1 (over z), sp: 8 (over y, x, core).
Axes of the slice: x: 2, y: 2, z: 1, core: 2. Of those that a mesh axis runs over, the one named last changes fastest.
Arguments:
- resid: float32 [32, 2048, 768], P('dp', 'sp')
- pre_norm: float32 [2, 768], replicated
- w_in: bfloat16 [2, 768, 3352], replicated
- conv_w: float32 [2, 1792, 4], replicated
- conv_b: float32 [2, 1792], replicated
- dt_bias: float32 [2, 24], replicated
- a_log: float32 [2, 24], replicated
- d_skip: float32 [2, 24], replicated
- gate_norm: float32 [2, 1, 1536], replicated
- w_out: bfloat16 [2, 1536, 768], replicated
Outputs:
- output 1: float32 [32, 2048, 768], P('dp', 'sp')
- output 2: float32 [32, 2, 24, 64, 128], P('dp', None, 'sp')
- output 3: bfloat16 [32, 2, 1792, 3], P('dp')
All inputs are finite; a program needn't handle non-finite values.
Results may differ from a plain program's by a relative error of at most 0.0179264.
Values are sent between devices in bfloat16 or wider.
A program may use at most 1 GiB of HBM per device.

v0:
```python
import jax
import jax.numpy as jnp
from jax import lax
from jax.sharding import PartitionSpec as P

CONV_WIDTH = 4
CHUNK = 256
EPSILON = 1e-5


def rms_norm(values, gain_vec):
    mean_sq = jnp.mean(values * values, axis=-1, keepdims=True)
    return values * lax.rsqrt(mean_sq + EPSILON) * gain_vec


def ssd_scan(x_in, dt_in, bc_in, a_neg, d_vec):
    batch, seq_len, groups, per_group, head_dim = x_in.shape
    d_state = bc_in.shape[-1]
    causal = jnp.arange(CHUNK)[:, None] >= jnp.arange(CHUNK)[None, :]

    def body(chunk_index, carry):
        state, y_buffer = carry
        start = chunk_index * CHUNK
        x_chunk = lax.dynamic_slice_in_dim(x_in, start, CHUNK, axis=1)
        dt_chunk = lax.dynamic_slice_in_dim(dt_in, start, CHUNK, axis=1).astype(jnp.float32)
        bc_chunk = lax.dynamic_slice_in_dim(bc_in, start, CHUNK, axis=1)
        b_chunk = bc_chunk[:, :, 0]
        c_chunk = bc_chunk[:, :, 1]
        cum_log = jnp.cumsum(dt_chunk * a_neg, axis=1)
        cum_heads = jnp.transpose(cum_log, (0, 2, 3, 1))
        log_diff = cum_heads[..., :, None] - cum_heads[..., None, :]
        decay_mat = jnp.exp(jnp.where(causal, log_diff, -jnp.inf))
        scores = jnp.einsum('btgn,bsgn->bgts', c_chunk, b_chunk, preferred_element_type=jnp.float32)
        mix_mat = decay_mat * scores[:, :, None]
        x_float = x_chunk.astype(jnp.float32)
        x_scaled = x_float * dt_chunk[..., None]
        y_intra = jnp.einsum('bghts,bsghp->btghp', mix_mat, x_scaled, preferred_element_type=jnp.float32)
        y_inter = jnp.einsum('btgn,bghpn->btghp', c_chunk.astype(jnp.float32), state, preferred_element_type=jnp.float32)
        to_end = jnp.exp(cum_log[:, -1:] - cum_log)
        state = state * jnp.exp(cum_log[:, -1])[..., None, None] + jnp.einsum('bsghp,bsgn->bghpn', x_scaled * to_end[..., None], b_chunk.astype(jnp.float32), preferred_element_type=jnp.float32)
        y_chunk = y_intra + y_inter * jnp.exp(cum_log)[..., None] + d_vec[:, :, None] * x_float
        y_buffer = lax.dynamic_update_slice_in_dim(y_buffer, y_chunk.astype(jnp.bfloat16), start, axis=1)
        return state, y_buffer

    state_zero = jnp.zeros((batch, groups, per_group, head_dim, d_state), jnp.float32)
    y_zero = jnp.zeros(x_in.shape, jnp.bfloat16)
    return lax.fori_loop(0, seq_len // CHUNK, body, (state_zero, y_zero))


def solution(mesh):
    seg_count = mesh.shape['sp']

    def layer(resid, pre_w, w_in_l, conv_w_l, conv_b_l, dt_b, a_log_l, d_l, gate_w, w_out_l):
        batch, seg_len, d_model = resid.shape
        n_groups, group_width = gate_w.shape
        d_inner = n_groups * group_width
        n_heads = dt_b.shape[0]
        conv_dim = conv_b_l.shape[0]
        d_state = (conv_dim - d_inner) // (2 * n_groups)
        head_dim = d_inner // n_heads
        seq_len = seg_len * seg_count
        local_heads = n_heads // seg_count
        local_groups = max(n_groups // seg_count, 1)
        local_per_group = local_heads // local_groups
        repeat_count = max(seg_count // n_groups, 1)
        seg_index = lax.axis_index('sp')

        normed = rms_norm(resid, pre_w).astype(jnp.bfloat16)
        projected = jnp.einsum('bld,de->ble', normed, w_in_l, preferred_element_type=jnp.float32).astype(jnp.bfloat16)
        gate_z = projected[..., :d_inner]
        xbc = projected[..., d_inner:d_inner + conv_dim]
        dt_raw = projected[..., d_inner + conv_dim:]
        halo_rows = lax.ppermute(xbc[:, seg_len - (CONV_WIDTH - 1):], 'sp', [(source, source + 1) for source in range(seg_count - 1)])
        padded = jnp.concatenate([halo_rows, xbc], axis=1)
        conv_out = conv_b_l + sum(padded[:, tap_index:tap_index + seg_len].astype(jnp.float32) * conv_w_l[:, tap_index] for tap_index in range(CONV_WIDTH))
        activated = jax.nn.silu(conv_out).astype(jnp.bfloat16)
        delta = jax.nn.softplus(dt_raw.astype(jnp.float32) + dt_b).astype(jnp.bfloat16)
        bc_tokens = jnp.repeat(activated[..., d_inner:].reshape(batch, seg_len, 2, n_groups, d_state), repeat_count, axis=3)

        x_local = lax.all_to_all(activated[..., :d_inner], 'sp', 2, 1, tiled=True)
        dt_local = lax.all_to_all(delta, 'sp', 2, 1, tiled=True)
        bc_local = lax.all_to_all(bc_tokens, 'sp', 3, 1, tiled=True)

        head_start = seg_index * local_heads
        a_neg = -jnp.exp(lax.dynamic_slice_in_dim(a_log_l, head_start, local_heads)).reshape(local_groups, local_per_group)
        d_local = lax.dynamic_slice_in_dim(d_l, head_start, local_heads).reshape(local_groups, local_per_group)
        final, y_local = ssd_scan(x_local.reshape(batch, seq_len, local_groups, local_per_group, head_dim), dt_local.reshape(batch, seq_len, local_groups, local_per_group), bc_local, a_neg, d_local)

        y_tokens = lax.all_to_all(y_local.reshape(batch, seq_len, local_heads * head_dim), 'sp', 1, 2, tiled=True)

        gated = y_tokens.reshape(batch, seg_len, n_groups, group_width).astype(jnp.float32) * jax.nn.silu(gate_z.reshape(batch, seg_len, n_groups, group_width).astype(jnp.float32))
        normed_y = (gated * lax.rsqrt(jnp.mean(gated * gated, axis=-1, keepdims=True) + EPSILON) * gate_w).astype(jnp.bfloat16)
        out_proj = jnp.einsum('blgc,gcd->bld', normed_y, w_out_l.reshape(n_groups, group_width, d_model), preferred_element_type=jnp.float32)
        tail_rows = jnp.where(seg_index == seg_count - 1, xbc[:, seg_len - (CONV_WIDTH - 1):], jnp.zeros((), jnp.bfloat16))
        conv_state = lax.psum(tail_rows, 'sp')
        return resid + out_proj, final.reshape(batch, local_heads, head_dim, d_state), jnp.swapaxes(conv_state, 1, 2)

    def forward(resid, pre_norm, w_in, conv_w, conv_b, dt_bias, a_log, d_skip, gate_norm, w_out):
        finals = []
        tails = []
        for layer_index in range(w_in.shape[0]):
            resid, final, tail_rows = layer(resid, pre_norm[layer_index], w_in[layer_index], conv_w[layer_index], conv_b[layer_index], dt_bias[layer_index], a_log[layer_index], d_skip[layer_index], gate_norm[layer_index], w_out[layer_index])
            finals.append(final)
            tails.append(tail_rows)
        return resid, jnp.stack(finals, axis=1), jnp.stack(tails, axis=1)

    return jax.shard_map(forward, mesh=mesh, in_specs=(P('dp', 'sp', None), P(), P(), P(), P(), P(), P(), P(), P(), P()), out_specs=(P('dp', 'sp', None), P('dp', None, 'sp', None, None), P('dp', None, None, None)), check_vma=False)
```

profile of v0, /device:TPU:0, one launch (start us, length us, event | category | flops | bytes accessed | tf_op | source)
XLA Modules:
  0.0 4124.6 jit_solution(6477451647023267029)
XLA Ops:
  8.5 10.2 multiply_reduce_fusion.3
  18.8 51.7 %convolution_convert_fusion.1 = bf16[32,256,3352]{1,2,0:T(8,128)(2,1)} fusion(f32[32,256,768]{2,1,0:T(8,128)} %param.14, f32[768]{0:T(1024)S(1)} %get-tuple-element.457, f32[32,256]{1,0:T(8,128)S(1)} %add_rsqrt_fusion.3, bf16[2,768,3352]{1,2,0:T(8,128)(2,1)} %param.16), kind=kOutput, calls=%fused_computation.143 | convolution fusion | flops 42224254976 | bytes 85269504 | tf_op jit(solution)/shard_map/bld,de->ble/dot_general | solution.py:69
  70.5 17.0 select_bitcast_fusion.1
  87.5 11.7 copy.327
  109.7 20.2 slice.262
  130.6 9.8 copy.328
  140.4 74.1 %multiply_convert_fusion.1 = bf16[32,256,1792]{1,2,0:T(8,128)(2,1)} fusion(bf16[32,256,1792]{1,2,0:T(8,128)(2,1)} %slice.262, bf16[32,3,1792]{1,2,0:T(8,128)(2,1)} %copy.328, f32[1792]{0:T(1024)S(1)} %get-tuple-element.449, f32[1792]{0:T(1024)S(1)} %get-tuple-element.450, f32[1792]{0:T(1024)S(1)} %get-tuple-element.451, f32[1792]{0:T(1024)S(1)} %get-tuple-element.448, ...), kind=kLoop, calls=%fused_computation.121 | loop fusion | flops 381681664 | bytes 59100160 | tf_op jit(solution)/shard_map/convert_element_type | solution.py:76
  222.6 45.5 %copy.329 = bf16[32,256,1536]{1,0,2:T(8,128)(2,1)} copy(bf16[32,256,1536]{1,2,0:T(8,128)(2,1)S(1)} %slice-done) | data formatting | bytes 50331648 | tf_op jit(solution)/shard_map/slice | solution.py:80
  284.3 262.9 %all-to-all-done.1 = bf16[32,256,1536]{1,0,2:T(8,128)(2,1)} async-done(((bf16[32,256,1536]{1,0,2:T(8,128)(2,1)}), bf16[32,256,1536]{1,0,2:T(8,128)(2,1)}, u32[]{:S(2)}, u32[]{:S(2)}) %all-to-all-start.1) | async-done | bytes 25165856 | tf_op jit(solution)/shard_map/all_to_all | solution.py:80
  547.2 12.7 reshape.535
  570.2 25.9 copy.330
  596.2 37.8 reshape.533
  634.0 295.9 %all-to-all-done.2 = bf16[32,256,2,8,128]{4,1,0,2,3:T(8,128)(2,1)} async-done(((bf16[32,256,2,8,128]{4,1,0,2,3:T(8,128)(2,1)}), bf16[32,256,2,8,128]{4,1,0,2,3:T(8,128)(2,1)}, u32[]{:S(2)}, u32[]{:S(2)}) %all-to-all-start.2) | async-done | bytes 33554464 | tf_op jit(solution)/shard_map/all_to_all | solution.py:82
  929.9 22.8 copy.332
  961.3 273.9 %while.32 = (s32[]{:T(128)}, f32[32,1,3,64,128]{4,3,2,0,1:T(8,128)S(1)}, bf16[32,2048,1,3,64]{1,4,3,0,2:T(8,128)(2,1)}, bf16[32,2048,1,3]{1,0,3,2:T(8,128)(2,1)}...) while((s32[]{:T(128)}, ...), condition=%wide.region_4.5_spmd.clone, body=%wide.region_1.4_spmd.clone.sunk | while | flops 2190139648 | bytes 64242548 | solution.py:47
  971.6 9.2 fusion.196
  1005.9 9.1 fusion.196
  1040.1 9.2 fusion.196
  1074.4 9.1 fusion.196
  1108.6 9.2 fusion.196
  1142.8 9.1 fusion.196
  1177.1 9.1 fusion.196
  1211.3 9.1 fusion.196
  1235.3 48.4 %copy.334 = bf16[32,2048,192]{2,0,1:T(8,128)(2,1)} copy(bf16[32,2048,192]{1,2,0:T(8,128)(2,1)} %bitcast.359) | data formatting | bytes 50331648 | tf_op jit(solution)/shard_map/reshape | solution.py:89
  1290.5 363.3 %all-to-all-done.3 = bf16[32,2048,192]{2,0,1:T(8,128)(2,1)} async-done(((bf16[32,2048,192]{2,0,1:T(8,128)(2,1)}), bf16[32,2048,192]{2,0,1:T(8,128)(2,1)}, u32[]{:S(2)}, u32[]{:S(2)}) %all-to-all-start.3) | async-done | bytes 25165856 | tf_op jit(solution)/shard_map/all_to_all | solution.py:89
  1653.8 44.9 %copy.335 = bf16[32,2048,192]{1,2,0:T(8,128)(2,1)} copy(bf16[32,2048,192]{2,0,1:T(8,128)(2,1)} %all-to-all-done.3) | data formatting | bytes 50331648 | tf_op jit(solution)/shard_map/all_to_all | solution.py:89
  1698.7 27.4 convert_element_type.184
  1726.1 43.9 %copy.368 = f32[768,8,8,256]{3,2,1,0:T(8,128)} copy(f32[768,8,8,256]{3,1,2,0:T(8,128)} %bitcast.352) | data formatting | bytes 100663296
  1770.0 45.3 %copy.336 = f32[32,256,8,192]{1,3,2,0:T(8,128)} copy(f32[32,256,8,192]{1,2,3,0:T(8,128)} %bitcast.353) | data formatting | bytes 100663296 | tf_op jit(solution)/shard_map/convert_element_type | solution.py:91
  1815.3 40.6 multiply_reduce_fusion.1
  1855.9 38.6 multiply_reduce_fusion.2
  1894.5 52.1 %convolution_convert_fusion = bf16[32,256,3352]{1,2,0:T(8,128)(2,1)} fusion(f32[32,256,768]{2,1,0:T(8,128)} %get-tuple-element.513, f32[768]{0:T(1024)S(1)} %copy-done.9, f32[32,256]{1,0:T(8,128)S(1)} %add_rsqrt_fusion.1, bf16[2,768,3352]{1,2,0:T(8,128)(2,1)} %param.16), kind=kOutput, calls=%fused_computation.142 | convolution fusion | flops 42224254976 | bytes 85269504 | tf_op jit(solution)/shard_map/bld,de->ble/dot_general | solution.py:69
  1946.6 16.9 select_bitcast_fusion
  1963.5 11.7 copy.340
  1976.6 20.2 slice.276
  2001.7 9.8 copy.341
  2011.6 74.3 %multiply_convert_fusion = bf16[32,256,1792]{1,2,0:T(8,128)(2,1)} fusion(bf16[32,256,1792]{1,2,0:T(8,128)(2,1)} %slice.276, bf16[32,3,1792]{1,2,0:T(8,128)(2,1)} %copy.341, f32[1792]{0:T(1024)S(1)} %get-tuple-element.445, f32[1792]{0:T(1024)S(1)} %get-tuple-element.446, f32[1792]{0:T(1024)S(1)} %get-tuple-element.447, f32[1792]{0:T(1024)S(1)} %get-tuple-element.444, ...), kind=kLoop, calls=%fused_computation.120 | loop fusion | flops 381681664 | bytes 59100160 | tf_op jit(solution)/shard_map/convert_element_type | solution.py:76
  2094.0 45.5 %copy.342 = bf16[32,256,1536]{1,0,2:T(8,128)(2,1)} copy(bf16[32,256,1536]{1,2,0:T(8,128)(2,1)S(1)} %slice-done.1) | data formatting | bytes 50331648 | tf_op jit(solution)/shard_map/slice | solution.py:80
  2155.7 262.9 %all-to-all-done.5 = bf16[32,256,1536]{1,0,2:T(8,128)(2,1)} async-done(((bf16[32,256,1536]{1,0,2:T(8,128)(2,1)}), bf16[32,256,1536]{1,0,2:T(8,128)(2,1)}, u32[]{:S(2)}, u32[]{:S(2)}) %all-to-all-start.5) | async-done | bytes 25165856 | tf_op jit(solution)/shard_map/all_to_all | solution.py:80
  2418.6 12.7 reshape.541
  2440.4 26.0 copy.343
  2466.3 37.8 reshape.539
  2504.1 297.1 %all-to-all-done.6 = bf16[32,256,2,8,128]{4,1,0,2,3:T(8,128)(2,1)} async-done(((bf16[32,256,2,8,128]{4,1,0,2,3:T(8,128)(2,1)}), bf16[32,256,2,8,128]{4,1,0,2,3:T(8,128)(2,1)}, u32[]{:S(2)}, u32[]{:S(2)}) %all-to-all-start.6) | async-done | bytes 33554464 | tf_op jit(solution)/shard_map/all_to_all | solution.py:82
  2801.2 22.8 copy.345
  2824.0 8.7 broadcast.177
  2832.7 274.6 %while.33 = (s32[]{:T(128)}, f32[32,1,3,64,128]{4,3,2,0,1:T(8,128)S(1)}, bf16[32,2048,1,3,64]{1,4,3,0,2:T(8,128)(2,1)}, bf16[32,2048,1,3]{1,0,3,2:T(8,128)(2,1)}...) while((s32[]{:T(128)}, ...), condition=%wide.region_10.11_spmd.clone, body=%wide.region_7.10_spmd.clone.sunk | while | flops 2190139648 | bytes 64242548 | solution.py:47
  2842.9 9.2 fusion.208
  2877.3 9.1 fusion.208
  2911.6 9.2 fusion.208
  2946.0 9.1 fusion.208
  2980.3 9.2 fusion.208
  3014.7 9.1 fusion.208
  3049.0 9.1 fusion.208
  3083.2 9.1 fusion.208
  3107.3 48.4 %copy.347 = bf16[32,2048,192]{2,0,1:T(8,128)(2,1)} copy(bf16[32,2048,192]{1,2,0:T(8,128)(2,1)} %bitcast.358) | data formatting | bytes 50331648 | tf_op jit(solution)/shard_map/reshape | solution.py:89
  3162.4 683.7 %all-reduce.3.cloned.1.call-done = (bf16[32,1,1792,3]{3,2,0,1:T(8,128)(2,1)}, bf16[32,1,1792,3]{3,2,0,1:T(8,128)(2,1)}) async-done(((bf16[32,1,1792,3]{3,2,0,1:T(8,128)(2,1)}, bf16[32,1,1792,3]{3,2,0,1:T(8,128)(2,1)}), (bf16[32,1,1792,3]{3,2,0,1:T(8,128)(2,1)}, bf16[32,1,1792,3]{3,2,0,1:T(8,128)(2,1)})) %all-reduce.3.cloned.1.call-update) | async-done | bytes 688144 | tf_op jit(solution)/shard_map/psum | solution.py:95
  3846.0 12.1 copy.353
  3858.1 12.2 copy.354
  3878.4 44.9 %copy.348 = bf16[32,2048,192]{1,2,0:T(8,128)(2,1)} copy(bf16[32,2048,192]{2,0,1:T(8,128)(2,1)} %all-to-all-done.7) | data formatting | bytes 50331648 | tf_op jit(solution)/shard_map/all_to_all | solution.py:89
  3923.3 27.4 convert_element_type.185
  3950.7 43.9 %copy.369 = f32[768,8,8,256]{3,2,1,0:T(8,128)} copy(f32[768,8,8,256]{3,1,2,0:T(8,128)} %bitcast.354) | data formatting | bytes 100663296
  3994.6 45.3 %copy.349 = f32[32,256,8,192]{1,3,2,0:T(8,128)} copy(f32[32,256,8,192]{1,2,3,0:T(8,128)} %bitcast.355) | data formatting | bytes 100663296 | tf_op jit(solution)/shard_map/convert_element_type | solution.py:91
  4039.8 40.6 multiply_reduce_fusion
  4080.4 37.1 fusion.132
  (568 shorter events, 517.4 us)
Async XLA Ops:
  70.5 31.4 copy-start.11
  70.5 38.6 copy-start.4
  99.1 31.5 collective-permute-start
  104.9 163.2 %all-to-all-start = ((bf16[32,256,24]{1,0,2:T(8,128)(2,1)}), bf16[32,256,24]{1,0,2:T(8,128)(2,1)S(1)}, u32[]{:S(2)}, u32[]{:S(2)}) async-start(bf16[32,256,24]{1,0,2:T(8,128)(2,1)} %copy.325), calls=%async_computation | async-start | bytes 786432 | tf_op jit(solution)/shard_map/all_to_all | solution.py:81
  109.7 20.2 copy-start.6
  214.5 8.2 slice-start
  268.1 279.1 %all-to-all-start.1 = ((bf16[32,256,1536]{1,0,2:T(8,128)(2,1)}), bf16[32,256,1536]{1,0,2:T(8,128)(2,1)}, u32[]{:S(2)}, u32[]{:S(2)}) async-start(bf16[32,256,1536]{1,0,2:T(8,128)(2,1)} %copy.329), calls=%async_computation.1 | async-start | bytes 50331648 | tf_op jit(solution)/shard_map/all_to_all | solution.py:80
  559.8 6.2 copy-start.12
  559.8 6.8 copy-start.13
  559.8 370.1 %all-to-all-start.2 = ((bf16[32,256,2,8,128]{4,1,0,2,3:T(8,128)(2,1)}), bf16[32,256,2,8,128]{4,1,0,2,3:T(8,128)(2,1)}, u32[]{:S(2)}, u32[]{:S(2)}) async-start(bf16[32,256,2,8,128]{4,1,0,2,3:T(8,128)(2,1)} %reshape.535), calls=%async_computation.2 | async-start | bytes 67108864 | tf_op jit(solution)/shard_map/all_to_all | solution.py:82
  1235.2 48.5 %copy-start = (f32[32,1,3,64,128]{4,3,2,0,1:T(8,128)}, f32[32,1,3,64,128]{4,3,2,0,1:T(8,128)S(1)}, u32[]{:S(2)}) copy-start(f32[32,1,3,64,128]{4,3,2,0,1:T(8,128)S(1)} %get-tuple-element.315) | copy-start | bytes 9437188
  1283.7 6.2 copy-start.7
  1283.7 370.1 %all-to-all-start.3 = ((bf16[32,2048,192]{2,0,1:T(8,128)(2,1)}), bf16[32,2048,192]{2,0,1:T(8,128)(2,1)}, u32[]{:S(2)}, u32[]{:S(2)}) async-start(bf16[32,2048,192]{2,0,1:T(8,128)(2,1)} %copy.334), calls=%async_computation.3 | async-start | bytes 67108864 | tf_op jit(solution)/shard_map/all_to_all | solution.py:89
  1855.8 38.6 copy-start.9
  1946.6 29.9 copy-start.3
  1975.2 26.5 collective-permute-start.1
  1976.6 20.2 copy-start.10
  1976.6 35.0 copy-start.5
  1999.2 140.3 %all-to-all-start.4 = ((bf16[32,256,24]{1,0,2:T(8,128)(2,1)}), bf16[32,256,24]{1,0,2:T(8,128)(2,1)S(1)}, u32[]{:S(2)}, u32[]{:S(2)}) async-start(bf16[32,256,24]{1,0,2:T(8,128)(2,1)} %copy.338), calls=%async_computation.4 | async-start | bytes 786432 | tf_op jit(solution)/shard_map/all_to_all | solution.py:81
  2085.8 8.2 slice-start.1
  2139.5 279.1 %all-to-all-start.5 = ((bf16[32,256,1536]{1,0,2:T(8,128)(2,1)}), bf16[32,256,1536]{1,0,2:T(8,128)(2,1)}, u32[]{:S(2)}, u32[]{:S(2)}) async-start(bf16[32,256,1536]{1,0,2:T(8,128)(2,1)} %copy.342), calls=%async_computation.5 | async-start | bytes 50331648 | tf_op jit(solution)/shard_map/all_to_all | solution.py:80
  2431.2 6.1 copy-start.14
  2431.2 6.2 copy-start.15
  2431.2 370.0 %all-to-all-start.6 = ((bf16[32,256,2,8,128]{4,1,0,2,3:T(8,128)(2,1)}), bf16[32,256,2,8,128]{4,1,0,2,3:T(8,128)(2,1)}, u32[]{:S(2)}, u32[]{:S(2)}) async-start(bf16[32,256,2,8,128]{4,1,0,2,3:T(8,128)(2,1)} %reshape.541), calls=%async_computation.6 | async-start | bytes 67108864 | tf_op jit(solution)/shard_map/all_to_all | solution.py:82
  3107.3 48.5 %copy-start.2 = (f32[32,1,3,64,128]{4,3,2,0,1:T(8,128)}, f32[32,1,3,64,128]{4,3,2,0,1:T(8,128)S(1)}, u32[]{:S(2)}) copy-start(f32[32,1,3,64,128]{4,3,2,0,1:T(8,128)S(1)} %get-tuple-element.316) | copy-start | bytes 9437188
  3155.8 722.6 %all-to-all-start.7 = ((bf16[32,2048,192]{2,0,1:T(8,128)(2,1)}), bf16[32,2048,192]{2,0,1:T(8,128)(2,1)}, u32[]{:S(2)}, u32[]{:S(2)}) async-start(bf16[32,2048,192]{2,0,1:T(8,128)(2,1)} %copy.347), calls=%async_computation.7 | async-start | bytes 67108864 | tf_op jit(solution)/shard_map/all_to_all | solution.py:89
  3161.6 684.4 %all-reduce.3.cloned.1.call-start = ((), (), s32[]{:S(2)}) async-start(), calls=%async_computation.8 | async-start | bytes 58720256 | tf_op jit(solution)/shard_map/psum | solution.py:95
  3161.7 711.3 %copy-start.1 = (f32[32,1,3,64,128]{4,3,2,0,1:T(8,128)S(1)}, f32[32,1,3,64,128]{4,3,2,0,1:T(8,128)}, u32[]{:S(2)}) copy-start(f32[32,1,3,64,128]{4,3,2,0,1:T(8,128)} %copy-done) | copy-start | bytes 9437188
  4039.8 40.6 copy-start.8
Sparse Core Ops, SparseCore 0:
  3166.4 679.6 all-reduce.2
where the time goes:
time: 4150 us; the launch traced here: 4120 us
  waiting for transfers between devices  2170 us (52%)
  local copies, waits for them, and re-layouts  897 us (22%)
  matrix products  574 us (14%)
  other arithmetic  425 us (10%)
  starting transfers between devices  45.5 us (1%)
    psum x1, waiting for transfers between devices, layer(): conv_state = lax.psum(tail_rows, 'sp')  684 us
    all_to_all x2, waiting for transfers between devices, layer(): bc_local = lax.all_to_all(bc_tokens, 'sp', 3, 1, tiled=True)  593 us
    all_to_all x2, waiting for transfers between devices, layer(): x_local = lax.all_to_all(activated[..., :d_inner], 'sp', 2, 1, tiled=True)  526 us
    all_to_all x2, waiting for transfers between devices, layer(): lax.all_to_all(y_local.reshape(batch, seq_len, local_heads * head_dim), '...  363 us
    convert_element_type x2, other arithmetic, layer(): activated = jax.nn.silu(conv_out).astype(jnp.bfloat16)  148 us
    dot_general x16, matrix products, body(): jnp.einsum('bghts,bsghp->btghp', mix_mat, x_scaled, preferred_element_typ...  146 us
    dot_general x16, matrix products, body(): jnp.einsum('btgn,bghpn->btghp', c_chunk.astype(jnp.float32), state, prefe...  118 us
    slice x6, local copies, waits for them, and re-layouts, layer(): x_local = lax.all_to_all(activated[..., :d_inner], 'sp', 2, 1, tiled=True)  107 us
  transfers between devices with their start and end apart: 11, of which 6 were waited for; matrix products, arithmetic and copies ran while one was open for 12% of the time, Pallas kernels for 0%

commit v1 on v0

v1 whole, which is shorter than its diff:
```python
import functools

import jax
import jax.numpy as jnp
from jax import lax
from jax.experimental import pallas as pl
from jax.experimental.pallas import tpu as pltpu
from jax.sharding import PartitionSpec as P

EPSILON = 1e-5
HALO = 8
LANES = 128


def silu(v):
    half = 0.5 * v
    return half + half * jnp.tanh(half)


def softplus(v):
    return jnp.maximum(v, 0.0) + jnp.log1p(jnp.exp(-jnp.abs(v)))


def round_bf16(v):
    return v.astype(jnp.bfloat16).astype(jnp.float32)


def dot(a, b):
    return jnp.dot(a, b, preferred_element_type=jnp.float32)


def layer_kernel(dims, x_ref, pre_ref, w_in_ref, w_dt_ref, conv_w_ref, conv_b_ref, dtb_ref, a_ref, d_ref, gate_ref, w_out_ref, expand_ref,
                 out_ref, state_ref, tail_ref,
                 res_ref, u_ref, s_ref, g_ref, y_ref):
    d_model, d_inner, d_state, heads, seg, chunks = dims
    head_dim = d_inner // heads
    chunk = pl.program_id(0)
    layer = pl.program_id(1)
    quad = 256
    half = seg // 2

    @pl.when(chunk == 0)
    def _():
        u_ref[layer, :, 0:HALO, :] = jnp.zeros(u_ref.shape[1:2] + (HALO, LANES), jnp.float32)
        s_ref[layer] = jnp.zeros(s_ref.shape[1:], jnp.float32)

    @pl.when(chunk > 0)
    def _():
        u_ref[layer, :, 0:HALO, :] = u_ref[layer, :, seg:seg + HALO, :]

    @pl.when(layer == 0)
    def _():
        res_ref[...] = x_ref[0]

    resid = res_ref[...]
    mean_sq = jnp.mean(resid * resid, axis=-1, keepdims=True)
    h = (resid * lax.rsqrt(mean_sq + EPSILON) * pre_ref[layer]).astype(jnp.bfloat16)

    def conv(first_tile, count):
        outs = []
        for j in range(first_tile, first_tile + count):
            cols = slice(j * LANES, (j + 1) * LANES)
            acc = conv_b_ref[layer, :, cols] + u_ref[layer, j, HALO - 3:HALO - 3 + seg, :] * conv_w_ref[layer, 0:1, cols]
            for tap in range(1, 4):
                acc = acc + u_ref[layer, j, HALO - 3 + tap:HALO - 3 + tap + seg, :] * conv_w_ref[layer, tap:tap + 1, cols]
            outs.append(silu(acc).astype(jnp.bfloat16))
        return outs

    def project_conv(first_col):
        u = round_bf16(dot(h, w_in_ref[layer, :, d_inner + first_col:d_inner + first_col + quad]))
        first_tile = first_col // LANES
        for k in range(quad // LANES):
            u_ref[layer, first_tile + k, HALO:HALO + seg, :] = u[:, k * LANES:(k + 1) * LANES]
        return conv(first_tile, quad // LANES)

    dt_raw = round_bf16(dot(h, w_dt_ref[layer]))
    delta = softplus(dt_raw + dtb_ref[layer]).astype(jnp.bfloat16)
    b_act, c_act = project_conv(d_inner)

    rows = lax.broadcasted_iota(jnp.int32, (seg, seg), 0)
    columns = lax.broadcasted_iota(jnp.int32, (seg, seg), 1)
    tri = jnp.where(rows >= columns, 1.0, 0.0).astype(jnp.bfloat16)
    cum = dot(tri, delta) * a_ref[layer]
    cum_t = jnp.transpose(cum)

    scores = lax.dot_general(c_act, b_act, (((1,), (1,)), ((), ())), preferred_element_type=jnp.float32)
    scores = jnp.where(rows >= columns, scores, 0.0)
    scores_top = scores[:half, :half]
    scores_low = scores[half:, :half]
    scores_diag = scores[half:, half:]
    b_t = jnp.transpose(b_act.astype(jnp.float32)).astype(jnp.bfloat16)
    left = lax.broadcasted_iota(jnp.int32, (seg, LANES), 1) < head_dim

    sum_sq = jnp.zeros((seg, LANES), jnp.float32)
    for q in range(d_inner // quad):
        cols = slice(q * quad, (q + 1) * quad)
        x_tiles = project_conv(q * quad)
        x_act = jnp.concatenate(x_tiles, axis=1)
        z = round_bf16(dot(h, w_in_ref[layer, :, cols]))
        x_float = x_act.astype(jnp.float32)
        dt_wide = dot(delta, expand_ref[:, cols])
        x_scaled = x_float * dt_wide
        x_dot = x_scaled.astype(jnp.bfloat16)
        pair_cums = []
        y_heads = []
        for k in range(quad // LANES):
            pair = []
            for i in range(LANES // head_dim):
                head = (q * quad + k * LANES) // head_dim + i
                wide = jnp.broadcast_to(cum[:, head:head + 1], (seg, LANES))
                pair.append(wide)
                row = cum_t[head:head + 1, :]
                lane = k * LANES + i * head_dim
                m_top = jnp.exp(jnp.minimum(wide[:half] - row[:, :half], 0.0)) * scores_top
                m_low = jnp.exp(wide[half:] - row[:, :half]) * scores_low
                m_diag = jnp.exp(jnp.minimum(wide[half:] - row[:, half:], 0.0)) * scores_diag
                x_head = x_dot[:, lane:lane + head_dim]
                top = dot(m_top.astype(jnp.bfloat16), x_head[:half])
                low = dot(jnp.concatenate([m_low.astype(jnp.bfloat16), m_diag.astype(jnp.bfloat16)], axis=1), x_head)
                y_heads.append(jnp.concatenate([top, low], axis=0))
            pair_cums.append(jnp.where(left, pair[0], pair[1]))
        cum_wide = jnp.concatenate(pair_cums, axis=1)
        last = cum_wide[seg - 1:seg, :]
        state = s_ref[layer, :, cols]
        y_inter = dot(c_act, state.astype(jnp.bfloat16))
        y = jnp.concatenate(y_heads, axis=1) + y_inter * jnp.exp(cum_wide) + d_ref[layer, :, cols] * x_float
        x_end = (x_scaled * jnp.exp(last - cum_wide)).astype(jnp.bfloat16)
        s_ref[layer, :, cols] = state * jnp.exp(last) + dot(b_t, x_end)
        gated = round_bf16(y) * silu(z)
        g_ref[:, cols] = gated
        square = gated * gated
        for k in range(quad // LANES):
            sum_sq = sum_sq + square[:, k * LANES:(k + 1) * LANES]

    scale = lax.rsqrt(jnp.sum(sum_sq, axis=-1, keepdims=True) * (1.0 / d_inner) + EPSILON)
    normed = (g_ref[...] * scale * gate_ref[layer]).astype(jnp.bfloat16)
    result = resid + dot(normed, w_out_ref[layer])
    res_ref[...] = result

    @pl.when(layer == 1)
    def _():
        out_ref[0] = result

    @pl.when(chunk == chunks - 1)
    def _():
        tail_ref[layer] = u_ref[layer, :, seg:seg + HALO, :]
        per_device = d_inner // chunks
        final = jnp.transpose(s_ref[layer])
        for k in range(chunks):
            state_ref[k, layer] = final[k * per_device:(k + 1) * per_device, :]


def solution(mesh):
    seg_count = mesh.shape['sp']

    def forward(resid, pre_norm, w_in, conv_w, conv_b, dt_bias, a_log, d_skip, gate_norm, w_out):
        batch, seg, d_model = resid.shape
        layers, d_inner, _ = w_out.shape
        heads = dt_bias.shape[1]
        head_dim = d_inner // heads
        conv_dim = conv_b.shape[1]
        d_state = (conv_dim - d_inner) // 2
        tiles = conv_dim // LANES
        local_heads = heads // seg_count
        pieces = batch // seg_count

        pad = LANES - heads
        w_dt = jnp.pad(w_in[:, :, d_inner + conv_dim:], ((0, 0), (0, 0), (0, pad)))
        dtb = jnp.pad(dt_bias, ((0, 0), (0, pad)))[:, None]
        a_neg = jnp.pad(-jnp.exp(a_log), ((0, 0), (0, pad)))[:, None]
        d_wide = jnp.repeat(d_skip, head_dim, axis=1)[:, None]
        conv_w_t = jnp.swapaxes(conv_w, 1, 2)
        expand = (jnp.arange(LANES)[:, None] == jnp.arange(d_inner)[None, :] // head_dim).astype(jnp.bfloat16)
        params = (pre_norm[:, None], w_in, w_dt, conv_w_t, conv_b[:, None], dtb, a_neg, d_wide, gate_norm, w_out, expand)

        def whole(a):
            return pl.BlockSpec(a.shape, lambda c, l: (0,) * a.ndim, pipeline_mode=pl.Buffered(1))

        flops = 2 * seg * seg_count * layers * (d_model * w_in.shape[2] + d_inner * d_model + 4 * d_inner * seg)
        run = pl.pallas_call(
            functools.partial(layer_kernel, (d_model, d_inner, d_state, heads, seg, seg_count)),
            grid=(seg_count, layers),
            out_shape=(jax.ShapeDtypeStruct((seg_count, seg, d_model), jnp.float32),
                       jax.ShapeDtypeStruct((seg_count, layers, d_inner // seg_count, d_state), jnp.float32),
                       jax.ShapeDtypeStruct((layers, tiles, HALO, LANES), jnp.float32)),
            in_specs=[pl.BlockSpec((1, seg, d_model), lambda c, l: (c, 0, 0))] + [whole(a) for a in params],
            out_specs=(pl.BlockSpec((1, seg, d_model), lambda c, l: (c, 0, 0)),
                       pl.BlockSpec((seg_count, layers, d_inner // seg_count, d_state), lambda c, l: (0, 0, 0, 0)),
                       pl.BlockSpec((layers, tiles, HALO, LANES), lambda c, l: (0, 0, 0, 0))),
            scratch_shapes=[pltpu.VMEM((seg, d_model), jnp.float32),
                            pltpu.VMEM((layers, tiles, HALO + seg, LANES), jnp.float32),
                            pltpu.VMEM((layers, d_state, d_inner), jnp.float32),
                            pltpu.VMEM((seg, d_inner), jnp.float32),
                            pltpu.VMEM((8, LANES), jnp.float32)],
            compiler_params=pltpu.CompilerParams(dimension_semantics=('arbitrary', 'arbitrary'), vmem_limit_bytes=56 * 1024 * 1024),
            cost_estimate=pl.CostEstimate(flops=flops, bytes_accessed=4 * seg * seg_count * d_model * 2, transcendentals=0),
        )

        arrived = [lax.all_to_all(resid[i * seg_count:(i + 1) * seg_count], 'sp', 0, 0) for i in range(pieces)]
        outs, states, tails = [], [], []
        for i in range(pieces):
            out, state, tail = run(arrived[i], *params)
            outs.append(lax.all_to_all(out, 'sp', 0, 0))
            states.append(lax.all_to_all(state, 'sp', 0, 0))
            tails.append(jnp.swapaxes(tail[:, :, HALO - 3:], 2, 3).reshape(layers, conv_dim, 3).astype(jnp.bfloat16))
        result = jnp.concatenate(outs, axis=0)
        ssm_state = jnp.concatenate(states, axis=0).reshape(batch, layers, local_heads, head_dim, d_state)
        conv_state = lax.all_gather(jnp.stack(tails), 'sp', axis=1).reshape(batch, layers, conv_dim, 3)
        return result, ssm_state, conv_state

    return jax.shard_map(forward, mesh=mesh, in_specs=(P('dp', 'sp', None), P(), P(), P(), P(), P(), P(), P(), P(), P()), out_specs=(P('dp', 'sp', None), P('dp', None, 'sp', None, None), P('dp', None, None, None)), check_vma=False)
```

time: 4150 us -> 1090 us (0.26)
  waiting for transfers between devices: 2170 us -> 0.01 us
  local copies, waits for them, and re-layouts: 897 us -> 44.1 us
  matrix products: 574 us -> 0 us
  blocking collectives: 0 us -> 545 us
  Pallas kernels: 0 us -> 457 us
  other arithmetic: 425 us -> 22.9 us
    all_to_all x8 -> x5, waiting for transfers between devices: 1480 us -> 0.01 us  [the longest x3 0.01 us: forward(): states.append(lax.all_to_all(state, 'sp', 0, 0))]
    psum x1 -> x0, waiting for transfers between devices: 684 us -> none  [layer(): conv_state = lax.psum(tail_rows, 'sp')]
    dot_general x68 -> x0, matrix products: 574 us -> none  [the longest x16 146 us: body(): jnp.einsum('bghts,bsghp->btghp', mix_mat, x_scaled, preferred_element_typ...]
    all_to_all x0 -> x7, blocking collectives: none -> 472 us  [the longest x3 224 us: forward(): lax.all_to_all(resid[i * seg_count:(i + 1) * seg_count], 'sp', 0, 0)]
    pallas_call x0 -> x4, Pallas kernels: none -> 457 us  [forward(): out, state, tail = run(arrived[i], *params)]
    reshape x10 -> x1, local copies, waits for them, and re-layouts: 214 us -> 2.68 us  [forward(): lax.all_gather(jnp.stack(tails), 'sp', axis=1)]
    convert_element_type x6 -> x1, other arithmetic: 206 us -> 0.83 us  [forward(): (jnp.arange(LANES)[:, None] == jnp.arange(d_inner)[None, :] // head_dim)....]
    all_to_all x8 -> x0, local copies, waits for them, and re-layouts: 189 us -> none  [the longest x2 89.8 us: layer(): lax.all_to_all(y_local.reshape(batch, seq_len, local_heads * head_dim), '...]
  transfers between devices with their start and end apart: 11 -> 5, of which waited for: 6 -> 0; matrix products, arithmetic and copies ran while one was open for 12% -> 3% of each run, Pallas kernels for 0% -> 42%
where the time goes in v1:
time: 1090 us
  blocking collectives  545 us (50%)
  Pallas kernels  457 us (42%)
  local copies, waits for them, and re-layouts  44.1 us (4%)
  other arithmetic  22.9 us (2%)
  starting transfers between devices  16.2 us (1%)
    pallas_call x4, Pallas kernels, forward(): out, state, tail = run(arrived[i], *params)  457 us
    all_to_all x3, blocking collectives, forward(): lax.all_to_all(resid[i * seg_count:(i + 1) * seg_count], 'sp', 0, 0)  224 us
    all_to_all x3, blocking collectives, forward(): outs.append(lax.all_to_all(out, 'sp', 0, 0))  224 us
    all_gather x1, blocking collectives, forward(): lax.all_gather(jnp.stack(tails), 'sp', axis=1)  73.9 us
    all_to_all x1, blocking collectives, forward(): states.append(lax.all_to_all(state, 'sp', 0, 0))  23.7 us
  transfers between devices with their start and end apart: 5, of which 0 were waited for; matrix products, arithmetic and copies ran while one was open for 3% of the time, Pallas kernels for 42%

profile of v1, /device:TPU:0, one launch (start us, length us, event | category | flops | bytes accessed | tf_op | source)
XLA Modules:
  0.0 1086.5 jit_solution(9394591351454135961)
XLA Ops:
  0.6 15.7 %fusion.8 = (f32[8,256,768]{2,1,0:T(8,128)}, f32[8,256,768]{2,1,0:T(8,128)}, f32[8,256,768]{2,1,0:T(8,128)}, f32[8,256,768]{2,1,0:T(8,128)S(1)}) fusion(f32[32,256,768]{2,1,0:T(8,128)} %param.10), kind=kLoop, calls=%fused_computation.21 | loop fusion | bytes 50331648 | tf_op jit(solution)/shard_map/slice | solution.py:199
  16.3 0.0 copy-start
  16.3 76.9 %all_to_all.60.x_ref = f32[8,256,768]{2,1,0:T(8,128)} all-to-all(f32[8,256,768]{2,1,0:T(8,128)} %get-tuple-element.33), channel_id=1, replica_groups=mesh['dp'=1,'sp'=8] {'sp'}, dimensions={0} | all-to-all | bytes 12582912 | tf_op jit(solution)/shard_map/all_to_all | solution.py:199
  93.2 0.0 copy-done
  93.2 73.6 %all_to_all.61.x_ref = f32[8,256,768]{2,1,0:T(8,128)} all-to-all(f32[8,256,768]{2,1,0:T(8,128)S(1)} %copy-done), channel_id=1, replica_groups=mesh['dp'=1,'sp'=8] {'sp'}, dimensions={0} | all-to-all | bytes 12582912 | tf_op jit(solution)/shard_map/all_to_all | solution.py:199
  166.7 73.5 %all_to_all.62.x_ref = f32[8,256,768]{2,1,0:T(8,128)} all-to-all(f32[8,256,768]{2,1,0:T(8,128)S(1)} %get-tuple-element.36), channel_id=1, replica_groups=mesh['dp'=1,'sp'=8] {'sp'}, dimensions={0} | all-to-all | bytes 12582912 | tf_op jit(solution)/shard_map/all_to_all | solution.py:199
  240.3 0.0 copy-start.5
  240.3 0.0 copy-start.6
  240.3 0.0 copy-start.3
  240.3 0.0 copy-start.2
  240.3 0.0 copy-start.4
  240.3 3.7 all-to-all-start.6
  244.0 0.0 copy-done.5
  244.0 0.5 pad.12
  244.6 0.0 copy-done.6
  244.6 0.5 pad.13
  245.1 0.0 copy-done.3
  245.1 0.6 broadcast_in_dim.17.pre_ref
  245.7 0.0 copy-done.2
  245.7 0.6 broadcast_in_dim.18.conv_b_ref
  246.3 0.0 copy-done.4
  246.3 0.1 broadcast_in_dim.21
  246.4 0.7 broadcast_in_dim_reshape.3.d_ref
  247.1 13.7 %copy.30.w_in_ref = bf16[2,768,3352]{2,1,0:T(8,128)(2,1)} copy(bf16[2,768,3352]{1,2,0:T(8,128)(2,1)} %param.12) | data formatting | bytes 20594688 | tf_op args[2]
  260.8 1.0 slice.40
  261.8 0.8 pad.11.w_dt_ref
  262.7 0.8 fusion.expand_ref
  263.5 114.2 %shard_map.123 = (f32[8,256,768]{2,1,0:T(8,128)}, f32[8,2,192,128]{3,2,1,0:T(8,128)}, f32[2,14,8,128]{3,2,1,0:T(8,128)}) custom-call(f32[8,256,768]{2,1,0:T(8,128)} %all_to_all.62.x_ref, f32[2,1,768]{2,1,0:T(1,128)} %broadcast_in_dim.17.pre_ref, bf16[2,768,3352]{2,1,0:T(8,128)(2,1)} %copy.30.w_in_ref, bf16[2,768,128]{2,1,0:T(8,128)(2,1)} %pad.11.w_dt_ref, ...), custom_call_target="tpu_custom_call" | custom-call | flops 43637538816 | bytes 12582912 | tf_op jit(solution)/shard_map/pallas_call | solution.py:202
  377.7 0.0 all-to-all-done.6.x_ref
  377.7 2.8 all-to-all-start.10
  380.5 114.2 %shard_map.124 = (f32[8,256,768]{2,1,0:T(8,128)}, f32[8,2,192,128]{3,2,1,0:T(8,128)}, f32[2,14,8,128]{3,2,1,0:T(8,128)}) custom-call(f32[8,256,768]{2,1,0:T(8,128)} %all-to-all-done.6.x_ref, f32[2,1,768]{2,1,0:T(1,128)} %broadcast_in_dim.17.pre_ref, bf16[2,768,3352]{2,1,0:T(8,128)(2,1)} %copy.30.w_in_ref, bf16[2,768,128]{2,1,0:T(8,128)(2,1)} %pad.11.w_dt_ref, ...), custom_call_target="tpu_custom_call" | custom-call | flops 43637538816 | bytes 12582912 | tf_op jit(solution)/shard_map/pallas_call | solution.py:202
  494.7 0.0 all-to-all-done.10
  494.7 2.9 all-to-all-start.11
  497.6 114.3 %shard_map.122 = (f32[8,256,768]{2,1,0:T(8,128)}, f32[8,2,192,128]{3,2,1,0:T(8,128)}, f32[2,14,8,128]{3,2,1,0:T(8,128)}) custom-call(f32[8,256,768]{2,1,0:T(8,128)} %all_to_all.61.x_ref, f32[2,1,768]{2,1,0:T(1,128)} %broadcast_in_dim.17.pre_ref, bf16[2,768,3352]{2,1,0:T(8,128)(2,1)} %copy.30.w_in_ref, bf16[2,768,128]{2,1,0:T(8,128)(2,1)} %pad.11.w_dt_ref, ...), custom_call_target="tpu_custom_call" | custom-call | flops 43637538816 | bytes 12582912 | tf_op jit(solution)/shard_map/pallas_call | solution.py:202
  612.0 0.0 all-to-all-done.11
  612.0 3.3 all-to-all-start.9
  615.3 114.2 %shard_map.121 = (f32[8,256,768]{2,1,0:T(8,128)}, f32[8,2,192,128]{3,2,1,0:T(8,128)}, f32[2,14,8,128]{3,2,1,0:T(8,128)}) custom-call(f32[8,256,768]{2,1,0:T(8,128)} %all_to_all.60.x_ref, f32[2,1,768]{2,1,0:T(1,128)} %broadcast_in_dim.17.pre_ref, bf16[2,768,3352]{2,1,0:T(8,128)(2,1)} %copy.30.w_in_ref, bf16[2,768,128]{2,1,0:T(8,128)(2,1)} %pad.11.w_dt_ref, ...), custom_call_target="tpu_custom_call" | custom-call | flops 43637538816 | bytes 12582912 | tf_op jit(solution)/shard_map/pallas_call | solution.py:202
  729.5 0.0 all-to-all-done.9
  729.5 23.7 %all_to_all.63 = f32[8,2,192,128]{3,2,1,0:T(8,128)} all-to-all(f32[8,2,192,128]{3,2,1,0:T(8,128)} %get-tuple-element.19), channel_id=1, replica_groups=mesh['dp'=1,'sp'=8] {'sp'}, dimensions={0} | all-to-all | bytes 3145728 | tf_op jit(solution)/shard_map/all_to_all | solution.py:204
  753.2 0.0 copy-start.1
  753.2 0.0 slice-start
  753.2 76.7 %all_to_all.64 = f32[8,256,768]{2,1,0:T(8,128)} all-to-all(f32[8,256,768]{2,1,0:T(8,128)} %get-tuple-element.17), channel_id=1, replica_groups=mesh['dp'=1,'sp'=8] {'sp'}, dimensions={0} | all-to-all | bytes 12582912 | tf_op jit(solution)/shard_map/all_to_all | solution.py:203
  829.9 0.0 copy-done.1
  829.9 0.0 slice-start.1
  829.9 73.6 %all_to_all.65 = f32[8,256,768]{2,1,0:T(8,128)} all-to-all(f32[8,256,768]{2,1,0:T(8,128)S(1)} %copy-done.1), channel_id=1, replica_groups=mesh['dp'=1,'sp'=8] {'sp'}, dimensions={0} | all-to-all | bytes 12582912 | tf_op jit(solution)/shard_map/all_to_all | solution.py:203
  903.5 0.0 slice-done
  903.5 0.0 slice-done.1
  903.5 73.6 %all_to_all.66 = f32[8,256,768]{2,1,0:T(8,128)} all-to-all(f32[8,256,768]{2,1,0:T(8,128)S(1)} %bitcast.25), channel_id=1, replica_groups=mesh['dp'=1,'sp'=8] {'sp'}, dimensions={0} | all-to-all | bytes 12582912 | tf_op jit(solution)/shard_map/all_to_all | solution.py:203
  977.1 3.5 all-to-all-start.1
  980.6 0.9 fusion.3
  981.6 0.9 fusion.4
  982.6 0.9 fusion.2
  983.5 0.9 fusion.1
  984.5 0.2 pad_maximum_fusion.2
  984.7 73.9 %all-gather = bf16[4,16,1792,3]{2,0,3,1:T(4,128)(2,1)S(1)} all-gather(bf16[4,2,1792,3]{2,0,3,1:T(4,128)(2,1)S(1)} %copy.38), channel_id=2, replica_groups=mesh['dp'=1,'sp'=8] {'sp'}, dimensions={1}, use_global_device_ids=true | all-gather | bytes 774144 | tf_op jit(solution)/shard_map/all_gather | solution.py:208
  1058.6 0.9 copy.39
  1059.5 2.7 reshape.98
  1062.2 2.4 copy.40
  1064.6 4.3 pad_maximum_fusion.1
  1069.0 0.0 all-to-all-done.1
  1069.0 17.6 %pad_maximum_fusion = f32[32,256,768]{2,1,0:T(8,128)} fusion(f32[8,256,768]{2,1,0:T(8,128)} %all_to_all.65, f32[8,256,768]{2,1,0:T(8,128)} %all_to_all.64, f32[8,256,768]{2,1,0:T(8,128)} %all_to_all.66, f32[8,256,768]{2,1,0:T(8,128)} %all-to-all-done.1), kind=kLoop, calls=%fused_computation | loop fusion | flops 18874368 | bytes 50331648 | tf_op jit(solution)/shard_map/concatenate | solution.py:206
  (12 shorter events, 0.2 us)
Async XLA Ops:
  16.3 76.9 %copy-start = (f32[8,256,768]{2,1,0:T(8,128)S(1)}, f32[8,256,768]{2,1,0:T(8,128)}, u32[]{:S(2)}) copy-start(f32[8,256,768]{2,1,0:T(8,128)} %get-tuple-element.34) | copy-start | bytes 18874372
  240.3 3.7 copy-start.5
  240.3 4.3 copy-start.6
  240.3 4.8 copy-start.3
  240.3 5.4 copy-start.2
  240.3 6.0 copy-start.4
  240.3 137.4 %all-to-all-start.6 = ((f32[8,256,768]{2,1,0:T(8,128)}), f32[8,256,768]{2,1,0:T(8,128)}, u32[]{:S(2)}, u32[]{:S(2)}) async-start(f32[8,256,768]{2,1,0:T(8,128)} %get-tuple-element.35), calls=%async_computation.6 | async-start | bytes 12582912 | tf_op jit(solution)/shard_map/all_to_all | solution.py:199
  377.7 117.0 %all-to-all-start.10 = ((f32[8,2,192,128]{3,2,1,0:T(8,128)}), f32[8,2,192,128]{3,2,1,0:T(8,128)S(1)}, u32[]{:S(2)}, u32[]{:S(2)}) async-start(f32[8,2,192,128]{3,2,1,0:T(8,128)} %get-tuple-element.21), calls=%async_computation.10 | async-start | bytes 3145728 | tf_op jit(solution)/shard_map/all_to_all | solution.py:204
  494.7 117.3 %all-to-all-start.11 = ((f32[8,2,192,128]{3,2,1,0:T(8,128)}), f32[8,2,192,128]{3,2,1,0:T(8,128)S(1)}, u32[]{:S(2)}, u32[]{:S(2)}) async-start(f32[8,2,192,128]{3,2,1,0:T(8,128)} %get-tuple-element.22), calls=%async_computation.11 | async-start | bytes 3145728 | tf_op jit(solution)/shard_map/all_to_all | solution.py:204
  612.0 117.6 %all-to-all-start.9 = ((f32[8,2,192,128]{3,2,1,0:T(8,128)}), f32[8,2,192,128]{3,2,1,0:T(8,128)}, u32[]{:S(2)}, u32[]{:S(2)}) async-start(f32[8,2,192,128]{3,2,1,0:T(8,128)} %get-tuple-element.20), calls=%async_computation.9 | async-start | bytes 3145728 | tf_op jit(solution)/shard_map/all_to_all | solution.py:204
  753.2 76.7 %copy-start.1 = (f32[8,256,768]{2,1,0:T(8,128)S(1)}, f32[8,256,768]{2,1,0:T(8,128)}, u32[]{:S(2)}) copy-start(f32[8,256,768]{2,1,0:T(8,128)} %get-tuple-element.18) | copy-start | bytes 18874372
  753.2 150.3 %slice-start = ((s8[6291456]{0:T(1024)(128)(4,1)}), s8[4194304]{0:T(1024)(128)(4,1)S(1)}, s32[]{:S(2)}) async-start(s8[6291456]{0:T(1024)(128)(4,1)} %bitcast.24), calls=%async_computation.12 | async-start | bytes 8388608
  829.9 73.6 %slice-start.1 = ((s8[6291456]{0:T(1024)(128)(4,1)}), s8[2097152]{0:T(1024)(128)(4,1)S(1)}, s32[]{:S(2)}) async-start(s8[6291456]{0:T(1024)(128)(4,1)} %bitcast.24), calls=%async_computation.13 | async-start | bytes 4194304
  977.1 91.8 %all-to-all-start.1 = ((f32[8,256,768]{2,1,0:T(8,128)}), f32[8,256,768]{2,1,0:T(8,128)}, u32[]{:S(2)}, u32[]{:S(2)}) async-start(f32[8,256,768]{2,1,0:T(8,128)} %get-tuple-element.15), calls=%async_computation.1 | async-start | bytes 12582912 | tf_op jit(solution)/shard_map/all_to_all | solution.py:203

commit v2 on v1

--- a/solution.py
+++ b/solution.py
@@ -29,16 +29,84 @@
     return jnp.dot(a, b, preferred_element_type=jnp.float32)
 
 
-def layer_kernel(dims, x_ref, pre_ref, w_in_ref, w_dt_ref, conv_w_ref, conv_b_ref, dtb_ref, a_ref, d_ref, gate_ref, w_out_ref, expand_ref,
-                 out_ref, state_ref, tail_ref,
-                 res_ref, u_ref, s_ref, g_ref, y_ref):
-    d_model, d_inner, d_state, heads, seg, chunks = dims
+def forward_kernel(dims, x_hbm, w_in_hbm, w_out_hbm, pre_ref, w_dt_ref, conv_w_ref, conv_b_ref, dtb_ref, a_ref, d_ref, gate_ref, expand_ref,
+                   out_hbm, state_hbm, tail_ref,
+                   seg_ref, w_in_ref, w_out_ref, u_ref, s_ref, g_ref, stage_ref,
+                   w_sem, in_send, in_recv, out_send, out_recv, state_send, state_recv):
+    d_inner, heads, seg, chunks, pieces = dims
     head_dim = d_inner // heads
-    chunk = pl.program_id(0)
-    layer = pl.program_id(1)
+    piece = pl.program_id(0)
+    chunk = pl.program_id(1)
+    layer = pl.program_id(2)
+    me = lax.axis_index('sp')
     quad = 256
     half = seg // 2
 
+    def weight_copies(l):
+        return (pltpu.make_async_copy(w_in_hbm.at[l], w_in_ref.at[l], w_sem.at[0, l]),
+                pltpu.make_async_copy(w_out_hbm.at[l], w_out_ref.at[l], w_sem.at[1, l]))
+
+    def local_in(p):
+        return pltpu.make_async_copy(x_hbm.at[p * chunks + me], seg_ref.at[p, me], in_recv.at[p, me])
+
+    def send_in(p, peer):
+        return pltpu.make_async_remote_copy(src_ref=x_hbm.at[p * chunks + peer], dst_ref=seg_ref.at[p, me], send_sem=in_send.at[p, peer],
+                                            recv_sem=in_recv.at[p, me], device_id={'sp': peer}, device_id_type=pl.DeviceIdType.MESH)
+
+    def arrive_in(p, peer):
+        return pltpu.make_async_remote_copy(src_ref=x_hbm.at[p * chunks + me], dst_ref=seg_ref.at[p, peer], send_sem=in_send.at[p, peer],
+                                            recv_sem=in_recv.at[p, peer], device_id={'sp': peer}, device_id_type=pl.DeviceIdType.MESH)
+
+    def local_out(p):
+        return pltpu.make_async_copy(seg_ref.at[p, me], out_hbm.at[p * chunks + me], out_recv.at[p, me])
+
+    def send_out(p, peer):
+        return pltpu.make_async_remote_copy(src_ref=seg_ref.at[p, peer], dst_ref=out_hbm.at[p * chunks + me], send_sem=out_send.at[p, peer],
+                                            recv_sem=out_recv.at[p, me], device_id={'sp': peer}, device_id_type=pl.DeviceIdType.MESH)
+
+    def arrive_out(p, peer):
+        return pltpu.make_async_remote_copy(src_ref=seg_ref.at[p, me], dst_ref=out_hbm.at[p * chunks + peer], send_sem=out_send.at[p, peer],
+                                            recv_sem=out_recv.at[p, peer], device_id={'sp': peer}, device_id_type=pl.DeviceIdType.MESH)
+
+    def local_state(p, l):
+        return pltpu.make_async_copy(stage_ref.at[l, me], state_hbm.at[p * chunks + me, l], state_recv.at[p, l, me])
+
+    def send_state(p, l, peer):
+        return pltpu.make_async_remote_copy(src_ref=stage_ref.at[l, peer], dst_ref=state_hbm.at[p * chunks + me, l], send_sem=state_send.at[l, peer],
+                                            recv_sem=state_recv.at[p, l, me], device_id={'sp': peer}, device_id_type=pl.DeviceIdType.MESH)
+
+    def arrive_state(p, l, peer):
+        return pltpu.make_async_remote_copy(src_ref=stage_ref.at[l, me], dst_ref=state_hbm.at[p * chunks + peer, l], send_sem=state_send.at[l, peer],
+                                            recv_sem=state_recv.at[p, l, peer], device_id={'sp': peer}, device_id_type=pl.DeviceIdType.MESH)
+
+    @pl.when((piece == 0) & (chunk == 0) & (layer == 0))
+    def _():
+        barrier = pltpu.get_barrier_semaphore()
+        for k in range(1, chunks):
+            pl.semaphore_signal(barrier, inc=1, device_id={'sp': lax.rem(me + k, chunks)}, device_id_type=pl.DeviceIdType.MESH)
+        pl.semaphore_wait(barrier, chunks - 1)
+        for p in range(pieces):
+            local_in(p).start()
+            for k in range(1, chunks):
+                send_in(p, lax.rem(me + k, chunks)).start()
+            if p == 0:
+                for l in range(2):
+                    for copy in weight_copies(l):
+                        copy.start()
+
+    @pl.when((piece == 0) & (chunk == 0))
+    def _():
+        for copy in weight_copies(layer):
+            copy.wait()
+
+    @pl.when((layer == 0) & (chunk == me))
+    def _():
+        local_in(piece).wait()
+
+    @pl.when((layer == 0) & (chunk != me))
+    def _():
+        arrive_in(piece, chunk).wait_recv()
+
     @pl.when(chunk == 0)
     def _():
         u_ref[layer, :, 0:HALO, :] = jnp.zeros(u_ref.shape[1:2] + (HALO, LANES), jnp.float32)
@@ -48,11 +116,7 @@
     def _():
         u_ref[layer, :, 0:HALO, :] = u_ref[layer, :, seg:seg + HALO, :]
 
-    @pl.when(layer == 0)
-    def _():
-        res_ref[...] = x_ref[0]
-
-    resid = res_ref[...]
+    resid = seg_ref[piece, chunk]
     mean_sq = jnp.mean(resid * resid, axis=-1, keepdims=True)
     h = (resid * lax.rsqrt(mean_sq + EPSILON) * pre_ref[layer]).astype(jnp.bfloat16)
 
@@ -135,19 +199,48 @@
     scale = lax.rsqrt(jnp.sum(sum_sq, axis=-1, keepdims=True) * (1.0 / d_inner) + EPSILON)
     normed = (g_ref[...] * scale * gate_ref[layer]).astype(jnp.bfloat16)
     result = resid + dot(normed, w_out_ref[layer])
-    res_ref[...] = result
-
-    @pl.when(layer == 1)
-    def _():
-        out_ref[0] = result
+    seg_ref[piece, chunk] = result
+
+    @pl.when((layer == 1) & (chunk == me))
+    def _():
+        local_out(piece).start()
+
+    @pl.when((layer == 1) & (chunk != me))
+    def _():
+        send_out(piece, chunk).start()
+
+    @pl.when((chunk == chunks - 1) & (piece > 0))
+    def _():
+        local_state(piece - 1, layer).wait()
+        for k in range(1, chunks):
+            send_state(piece - 1, layer, lax.rem(me + k, chunks)).wait_send()
 
     @pl.when(chunk == chunks - 1)
     def _():
-        tail_ref[layer] = u_ref[layer, :, seg:seg + HALO, :]
+        tail_ref[0, layer] = u_ref[layer, :, seg:seg + HALO, :]
         per_device = d_inner // chunks
         final = jnp.transpose(s_ref[layer])
         for k in range(chunks):
-            state_ref[k, layer] = final[k * per_device:(k + 1) * per_device, :]
+            stage_ref[layer, k] = final[k * per_device:(k + 1) * per_device, :]
+        local_state(piece, layer).start()
+        for k in range(1, chunks):
+            send_state(piece, layer, lax.rem(me + k, chunks)).start()
+
+    @pl.when((piece == pieces - 1) & (chunk == chunks - 1) & (layer == 1))
+    def _():
+        for l in range(2):
+            local_state(pieces - 1, l).wait()
+        for p in range(pieces):
+            local_out(p).wait()
+            for k in range(1, chunks):
+                peer = lax.rem(me + k, chunks)
+                send_in(p, peer).wait_send()
+                send_out(p, peer).wait_send()
+                arrive_out(p, peer).wait_recv()
+                for l in range(2):
+                    arrive_state(p, l, peer).wait_recv()
+                    if p == pieces - 1:
+                        send_state(p, l, peer).wait_send()
 
 
 def solution(mesh):
@@ -171,41 +264,39 @@
         d_wide = jnp.repeat(d_skip, head_dim, axis=1)[:, None]
         conv_w_t = jnp.swapaxes(conv_w, 1, 2)
         expand = (jnp.arange(LANES)[:, None] == jnp.arange(d_inner)[None, :] // head_dim).astype(jnp.bfloat16)
-        params = (pre_norm[:, None], w_in, w_dt, conv_w_t, conv_b[:, None], dtb, a_neg, d_wide, gate_norm, w_out, expand)
+        params = (pre_norm[:, None], w_dt, conv_w_t, conv_b[:, None], dtb, a_neg, d_wide, gate_norm, expand)
 
         def whole(a):
-            return pl.BlockSpec(a.shape, lambda c, l: (0,) * a.ndim, pipeline_mode=pl.Buffered(1))
-
-        flops = 2 * seg * seg_count * layers * (d_model * w_in.shape[2] + d_inner * d_model + 4 * d_inner * seg)
-        run = pl.pallas_call(
-            functools.partial(layer_kernel, (d_model, d_inner, d_state, heads, seg, seg_count)),
-            grid=(seg_count, layers),
-            out_shape=(jax.ShapeDtypeStruct((seg_count, seg, d_model), jnp.float32),
-                       jax.ShapeDtypeStruct((seg_count, layers, d_inner // seg_count, d_state), jnp.float32),
-                       jax.ShapeDtypeStruct((layers, tiles, HALO, LANES), jnp.float32)),
-            in_specs=[pl.BlockSpec((1, seg, d_model), lambda c, l: (c, 0, 0))] + [whole(a) for a in params],
-            out_specs=(pl.BlockSpec((1, seg, d_model), lambda c, l: (c, 0, 0)),
-                       pl.BlockSpec((seg_count, layers, d_inner // seg_count, d_state), lambda c, l: (0, 0, 0, 0)),
-                       pl.BlockSpec((layers, tiles, HALO, LANES), lambda c, l: (0, 0, 0, 0))),
-            scratch_shapes=[pltpu.VMEM((seg, d_model), jnp.float32),
+            return pl.BlockSpec(a.shape, lambda p, c, l: (0,) * a.ndim, pipeline_mode=pl.Buffered(1))
+
+        hbm = pl.BlockSpec(memory_space=pl.ANY)
+        per_device = d_inner // seg_count
+        out, state, tail = pl.pallas_call(
+            functools.partial(forward_kernel, (d_inner, heads, seg, seg_count, pieces)),
+            grid=(pieces, seg_count, layers),
+            out_shape=(jax.ShapeDtypeStruct((batch, seg, d_model), jnp.float32),
+                       jax.ShapeDtypeStruct((batch, layers, per_device, d_state), jnp.float32),
+                       jax.ShapeDtypeStruct((pieces, layers, tiles, HALO, LANES), jnp.float32)),
+            in_specs=[hbm, hbm, hbm] + [whole(a) for a in params],
+            out_specs=(hbm, hbm, pl.BlockSpec((1, layers, tiles, HALO, LANES), lambda p, c, l: (p, 0, 0, 0, 0))),
+            scratch_shapes=[pltpu.VMEM((pieces, seg_count, seg, d_model), jnp.float32),
+                            pltpu.VMEM(w_in.shape, jnp.bfloat16),
+                            pltpu.VMEM(w_out.shape, jnp.bfloat16),
                             pltpu.VMEM((layers, tiles, HALO + seg, LANES), jnp.float32),
                             pltpu.VMEM((layers, d_state, d_inner), jnp.float32),
                             pltpu.VMEM((seg, d_inner), jnp.float32),
-                            pltpu.VMEM((8, LANES), jnp.float32)],
-            compiler_params=pltpu.CompilerParams(dimension_semantics=('arbitrary', 'arbitrary'), vmem_limit_bytes=56 * 1024 * 1024),
-            cost_estimate=pl.CostEstimate(flops=flops, bytes_accessed=4 * seg * seg_count * d_model * 2, transcendentals=0),
-        )
-
-        arrived = [lax.all_to_all(resid[i * seg_count:(i + 1) * seg_count], 'sp', 0, 0) for i in range(pieces)]
-        outs, states, tails = [], [], []
-        for i in range(pieces):
-            out, state, tail = run(arrived[i], *params)
-            outs.append(lax.all_to_all(out, 'sp', 0, 0))
-            states.append(lax.all_to_all(state, 'sp', 0, 0))
-            tails.append(jnp.swapaxes(tail[:, :, HALO - 3:], 2, 3).reshape(layers, conv_dim, 3).astype(jnp.bfloat16))
-        result = jnp.concatenate(outs, axis=0)
-        ssm_state = jnp.concatenate(states, axis=0).reshape(batch, layers, local_heads, head_dim, d_state)
-        conv_state = lax.all_gather(jnp.stack(tails), 'sp', axis=1).reshape(batch, layers, conv_dim, 3)
-        return result, ssm_state, conv_state
+                            pltpu.VMEM((layers, seg_count, per_device, d_state), jnp.float32),
+                            pltpu.SemaphoreType.DMA((2, layers)),
+                            pltpu.SemaphoreType.DMA((pieces, seg_count)),
+                            pltpu.SemaphoreType.DMA((pieces, seg_count)),
+                            pltpu.SemaphoreType.DMA((pieces, seg_count)),
+                            pltpu.SemaphoreType.DMA((pieces, seg_count)),
+                            pltpu.SemaphoreType.DMA((layers, seg_count)),
+                            pltpu.SemaphoreType.DMA((pieces, layers, seg_count))],
+            compiler_params=pltpu.CompilerParams(dimension_semantics=('arbitrary',) * 3, vmem_limit_bytes=67043328, collective_id=0, has_side_effects=True),
+        )(resid, w_in, w_out, *params)
+        tails = jnp.swapaxes(tail[:, :, :, HALO - 3:], 3, 4).reshape(pieces, layers, conv_dim, 3).astype(jnp.bfloat16)
+        conv_state = lax.all_gather(tails, 'sp', axis=1).reshape(batch, layers, conv_dim, 3)
+        return out, state.reshape(batch, layers, local_heads, head_dim, d_state), conv_state
 
     return jax.shard_map(forward, mesh=mesh, in_specs=(P('dp', 'sp', None), P(), P(), P(), P(), P(), P(), P(), P(), P()), out_specs=(P('dp', 'sp', None), P('dp', None, 'sp', None, None), P('dp', None, None, None)), check_vma=False)

time: 1090 us -> 704 us (0.65)
  blocking collectives: 545 us -> 39.2 us
  Pallas kernels: 457 us -> 618 us
  other arithmetic: 22.9 us -> 1.5 us
  starting transfers between devices: 16.2 us -> 0 us
    all_to_all x7 -> x0, blocking collectives: 472 us -> none  [the longest x3 224 us: forward(): lax.all_to_all(resid[i * seg_count:(i + 1) * seg_count], 'sp', 0, 0)]
    pallas_call x4 -> x1, Pallas kernels: 457 us -> 618 us  [forward(): pl.pallas_call(functools.partial(forward_kernel, (d_inner, heads, seg, se...]
    all_gather x1, blocking collectives: 73.9 us -> 39.2 us  [forward(): lax.all_gather(tails, 'sp', axis=1).reshape(batch, layers, conv_dim, 3)]
    concatenate x2 -> x0, other arithmetic: 21.9 us -> none  [the longest x1 17.6 us: forward(): result = jnp.concatenate(outs, axis=0)]
    unnamed x20 -> x8, local copies, waits for them, and re-layouts: 16.2 us -> 35.4 us
    all_to_all x5 -> x0, starting transfers between devices: 16.2 us -> none  [the longest x3 9.05 us: forward(): states.append(lax.all_to_all(state, 'sp', 0, 0))]
    slice x1 -> x0, local copies, waits for them, and re-layouts: 15.7 us -> none  [forward(): resid[i * seg_count:(i + 1) * seg_count]]
  transfers between devices with their start and end apart: 5 -> 0, of which waited for: 0 -> 0; matrix products, arithmetic and copies ran while one was open for 3% -> 0% of each run, Pallas kernels for 42% -> 0%
where the time goes in v2:
time: 704 us; the launch traced here: 703 us
  Pallas kernels  618 us (88%)
  local copies, waits for them, and re-layouts  44.4 us (6%)
  blocking collectives  39.2 us (6%)
    pallas_call x1, Pallas kernels, forward(): pl.pallas_call(functools.partial(forward_kernel, (d_inner, heads, seg, se...  618 us
    all_gather x1, blocking collectives, forward(): lax.all_gather(tails, 'sp', axis=1).reshape(batch, layers, conv_dim, 3)  39.2 us
    unnamed x8, local copies, waits for them, and re-layouts  35.4 us

profile of v2, /device:TPU:0, one launch (start us, length us, event | category | flops | bytes accessed | tf_op | source)
XLA Modules:
  0.0 703.3 jit_solution(7843580321421040261)
XLA Ops:
  0.6 1.3 pad.12
  1.9 0.7 exponential_negate_fusion
  2.6 0.6 pad.13
  3.2 1.3 broadcast_in_dim.17.pre_ref
  4.5 1.3 broadcast_in_dim.18.conv_b_ref
  5.8 0.7 broadcast_in_dim.21
  6.5 0.7 broadcast_in_dim_reshape.3.d_ref
  7.2 0.8 fusion.expand_ref
  8.0 13.7 %copy.24.w_in_hbm = bf16[2,768,3352]{2,1,0:T(8,128)(2,1)} copy(bf16[2,768,3352]{1,2,0:T(8,128)(2,1)} %param.12) | data formatting | bytes 20594688 | tf_op args[2]
  21.8 1.0 slice.9
  22.8 0.8 pad.11.w_dt_ref
  23.6 617.5 %shard_map.121 = (f32[32,256,768]{2,1,0:T(8,128)}, f32[32,2,192,128]{3,2,1,0:T(8,128)}, f32[4,2,14,8,128]{4,3,2,1,0:T(8,128)}) custom-call(f32[32,256,768]{2,1,0:T(8,128)} %x_hbm.1, bf16[2,768,3352]{2,1,0:T(8,128)(2,1)} %copy.24.w_in_hbm, bf16[2,1536,768]{2,1,0:T(8,128)(2,1)} %w_out_hbm.1, f32[2,1,768]{2,1,0:T(1,128)} %broadcast_in_dim.17.pre_ref, ...), custom_call_target="tpu_custom_call" | custom-call | tf_op jit(solution)/shard_map/pallas_call | solution.py:274
  641.1 1.1 fusion.1
  642.3 39.2 %all_gather.4 = bf16[4,8,2,1792,3]{3,0,4,2,1:T(4,128)(2,1)S(1)} all-gather(bf16[4,1,2,1792,3]{3,0,4,2,1:T(4,128)(2,1)S(1)} %reshape.63), channel_id=1, replica_groups=mesh['dp'=1,'sp'=8] {'sp'}, dimensions={1}, use_global_device_ids=true | all-gather | bytes 774144 | tf_op jit(solution)/shard_map/all_gather | solution.py:299
  681.4 0.1 copy.32
  681.6 0.0 slice-start
  681.6 1.6 copy.28
  683.1 0.0 slice-start.1
  683.1 17.4 %copy.35 = f32[32,256,768]{2,1,0:T(8,128)} copy(f32[32,256,768]{2,1,0:T(8,128)} %get-tuple-element.18) | data formatting | bytes 50331648
  700.6 0.0 slice-done
  700.6 0.0 slice-done.1
  700.6 2.7 copy.36
  (4 shorter events, 0.1 us)
Async XLA Ops:
  681.6 19.0 %slice-start = ((s8[6291456]{0:T(1024)(128)(4,1)}), s8[4194304]{0:T(1024)(128)(4,1)S(1)}, s32[]{:S(2)}) async-start(s8[6291456]{0:T(1024)(128)(4,1)} %bitcast.11), calls=%async_computation | async-start | bytes 8388608
  683.1 17.5 %slice-start.1 = ((s8[6291456]{0:T(1024)(128)(4,1)}), s8[2097152]{0:T(1024)(128)(4,1)S(1)}, s32[]{:S(2)}) async-start(s8[6291456]{0:T(1024)(128)(4,1)} %bitcast.11), calls=%async_computation.1 | async-start | bytes 4194304

commit v3 on v2

v3 whole, which is shorter than its diff:
```python
import functools

import jax
import jax.numpy as jnp
from jax import lax
from jax.experimental import pallas as pl
from jax.experimental.pallas import tpu as pltpu
from jax.sharding import PartitionSpec as P

EPSILON = 1e-5
HALO = 8
LANES = 128
LOG2_E = 1.4426950408889634


def softplus(v):
    return jnp.maximum(v, 0.0) + jnp.log1p(jnp.exp(-jnp.abs(v)))


def round_bf16(v):
    return v.astype(jnp.bfloat16).astype(jnp.float32)


def dot(a, b):
    return jnp.dot(a, b, preferred_element_type=jnp.float32)


def forward_kernel(dims, x_hbm, w_in_hbm, w_out_hbm, pre_ref, conv_w_ref, conv_b_ref, dt_bias_ref, a_log_ref, d_skip_ref, gate_ref,
                   out_hbm, state_hbm, tail_hbm,
                   seg_ref, w_in_ref, w_dt_ref, w_out_ref, raw_ref, row_ref, expand_ref, u_ref, s_ref, g_ref, stage_ref, tail_f_ref, tail_ref,
                   w_sem, raw_sem, in_send, in_recv, out_send, out_recv, state_send, state_recv, tail_send, tail_recv):
    d_inner, heads, seg, chunks, pieces = dims
    head_dim = d_inner // heads
    conv_dim = conv_b_ref.shape[1]
    tiles = conv_dim // LANES
    piece = pl.program_id(0)
    chunk = pl.program_id(1)
    layer = pl.program_id(2)
    me = lax.axis_index('sp')
    quad = 256
    sub = LANES
    blocks = (d_inner + conv_dim) // quad

    def raw_copy(l, j, slot):
        rows = pl.ds(pl.multiple_of(j * quad, quad), quad)
        return pltpu.make_async_copy(w_in_hbm.at[l, rows, :], raw_ref.at[slot], raw_sem.at[slot])

    def raw_dt_copy(l):
        return pltpu.make_async_copy(w_in_hbm.at[l, pl.ds(d_inner + conv_dim, heads), :], raw_ref.at[l, pl.ds(0, heads), :], raw_sem.at[l])

    def w_out_copy(l):
        return pltpu.make_async_copy(w_out_hbm.at[l], w_out_ref.at[l], w_sem.at[l])

    def local_tail(p):
        return pltpu.make_async_copy(tail_ref.at[p], tail_hbm.at[p * chunks + me], tail_recv.at[p, me])

    def send_tail(p, peer):
        return pltpu.make_async_remote_copy(src_ref=tail_ref.at[p], dst_ref=tail_hbm.at[p * chunks + me], send_sem=tail_send.at[p, peer],
                                            recv_sem=tail_recv.at[p, me], device_id={'sp': peer}, device_id_type=pl.DeviceIdType.MESH)

    def arrive_tail(p, peer):
        return pltpu.make_async_remote_copy(src_ref=tail_ref.at[p], dst_ref=tail_hbm.at[p * chunks + peer], send_sem=tail_send.at[p, peer],
                                            recv_sem=tail_recv.at[p, peer], device_id={'sp': peer}, device_id_type=pl.DeviceIdType.MESH)

    def local_in(p):
        return pltpu.make_async_copy(x_hbm.at[p * chunks + me], seg_ref.at[p, me], in_recv.at[p, me])

    def send_in(p, peer):
        return pltpu.make_async_remote_copy(src_ref=x_hbm.at[p * chunks + peer], dst_ref=seg_ref.at[p, me], send_sem=in_send.at[p, peer],
                                            recv_sem=in_recv.at[p, me], device_id={'sp': peer}, device_id_type=pl.DeviceIdType.MESH)

    def arrive_in(p, peer):
        return pltpu.make_async_remote_copy(src_ref=x_hbm.at[p * chunks + me], dst_ref=seg_ref.at[p, peer], send_sem=in_send.at[p, peer],
                                            recv_sem=in_recv.at[p, peer], device_id={'sp': peer}, device_id_type=pl.DeviceIdType.MESH)

    def local_out(p):
        return pltpu.make_async_copy(seg_ref.at[p, me], out_hbm.at[p * chunks + me], out_recv.at[p, me])

    def send_out(p, peer):
        return pltpu.make_async_remote_copy(src_ref=seg_ref.at[p, peer], dst_ref=out_hbm.at[p * chunks + me], send_sem=out_send.at[p, peer],
                                            recv_sem=out_recv.at[p, me], device_id={'sp': peer}, device_id_type=pl.DeviceIdType.MESH)

    def arrive_out(p, peer):
        return pltpu.make_async_remote_copy(src_ref=seg_ref.at[p, me], dst_ref=out_hbm.at[p * chunks + peer], send_sem=out_send.at[p, peer],
                                            recv_sem=out_recv.at[p, peer], device_id={'sp': peer}, device_id_type=pl.DeviceIdType.MESH)

    def local_state(p, l):
        return pltpu.make_async_copy(stage_ref.at[l, me], state_hbm.at[p * chunks + me, l], state_recv.at[p, l, me])

    def send_state(p, l, peer):
        return pltpu.make_async_remote_copy(src_ref=stage_ref.at[l, peer], dst_ref=state_hbm.at[p * chunks + me, l], send_sem=state_send.at[l, peer],
                                            recv_sem=state_recv.at[p, l, me], device_id={'sp': peer}, device_id_type=pl.DeviceIdType.MESH)

    def arrive_state(p, l, peer):
        return pltpu.make_async_remote_copy(src_ref=stage_ref.at[l, me], dst_ref=state_hbm.at[p * chunks + peer, l], send_sem=state_send.at[l, peer],
                                            recv_sem=state_recv.at[p, l, peer], device_id={'sp': peer}, device_id_type=pl.DeviceIdType.MESH)

    left = lax.broadcasted_iota(jnp.int32, (sub, LANES), 1) < head_dim

    @pl.when((piece == 0) & (chunk == 0) & (layer == 0))
    def _():
        for l in range(2):
            w_out_copy(l).start()
            raw_copy(0, l, l).start()
        barrier = pltpu.get_barrier_semaphore()
        for k in range(1, chunks):
            pl.semaphore_signal(barrier, inc=1, device_id={'sp': lax.rem(me + k, chunks)}, device_id_type=pl.DeviceIdType.MESH)
        pl.semaphore_wait(barrier, chunks - 1)
        for p in range(pieces):
            local_in(p).start()
            for k in range(1, chunks):
                send_in(p, lax.rem(me + k, chunks)).start()

        tail_f_ref[...] = jnp.zeros(tail_f_ref.shape, jnp.float32)
        row_ref[...] = jnp.zeros(row_ref.shape, jnp.float32)
        for l in range(2):
            for tap in range(4):
                row_ref[l, tap:tap + 1, 0:conv_dim] = 0.5 * conv_w_ref[l, tap:tap + 1, :]
            row_ref[l, 4:5, 0:conv_dim] = 0.5 * conv_b_ref[l:l + 1, :]
            row_ref[l, 5:6, 0:heads] = dt_bias_ref[l:l + 1, :]
            row_ref[l, 6:7, 0:heads] = -jnp.exp(a_log_ref[l:l + 1, :]) * LOG2_E
            for k in range(d_inner // LANES):
                d_left = jnp.broadcast_to(d_skip_ref[l:l + 1, 2 * k:2 * k + 1], (1, LANES))
                d_right = jnp.broadcast_to(d_skip_ref[l:l + 1, 2 * k + 1:2 * k + 2], (1, LANES))
                row_ref[l, 7:8, k * LANES:(k + 1) * LANES] = jnp.where(left[0:1], d_left, d_right)
        lane_head = lax.shift_right_logical(lax.broadcasted_iota(jnp.int32, expand_ref.shape, 1), 6)
        expand_ref[...] = jnp.where(lax.broadcasted_iota(jnp.int32, expand_ref.shape, 0) == lane_head, 1.0, 0.0).astype(jnp.bfloat16)

        for l in range(2):
            @pl.loop(0, blocks)
            def _(j):
                slot = lax.rem(j, 2)
                raw_copy(l, j, slot).wait()
                w_in_ref[l, :, pl.ds(pl.multiple_of(j * quad, quad), quad)] = jnp.transpose(raw_ref[slot])

                @pl.when(j + 2 < blocks)
                def _():
                    raw_copy(l, j + 2, slot).start()

            if l == 0:
                for j in range(2):
                    raw_copy(1, j, j).start()
        raw_ref[...] = jnp.zeros(raw_ref.shape, jnp.bfloat16)
        for l in range(2):
            raw_dt_copy(l).start()
        for l in range(2):
            raw_dt_copy(l).wait()
            w_dt_ref[l] = jnp.transpose(raw_ref[l, 0:LANES, :])
            w_out_copy(l).wait()

    @pl.when((layer == 0) & (chunk == me))
    def _():
        local_in(piece).wait()

    @pl.when((layer == 0) & (chunk != me))
    def _():
        arrive_in(piece, chunk).wait_recv()

    @pl.when(chunk == 0)
    def _():
        u_ref[layer, :, 0:HALO, :] = jnp.zeros(u_ref.shape[1:2] + (HALO, LANES), jnp.float32)
        s_ref[layer] = jnp.zeros(s_ref.shape[1:], jnp.float32)

    @pl.when(chunk > 0)
    def _():
        u_ref[layer, :, 0:HALO, :] = u_ref[layer, :, seg:seg + HALO, :]

    resid = seg_ref[piece, chunk]
    mean_sq = jnp.mean(resid * resid, axis=-1, keepdims=True)
    h = (resid * lax.rsqrt(mean_sq + EPSILON) * pre_ref[pl.ds(layer, 1), :]).astype(jnp.bfloat16)

    def project(first_col):
        u = round_bf16(dot(h, w_in_ref[layer, :, d_inner + first_col:d_inner + first_col + quad]))
        first_tile = first_col // LANES
        for k in range(quad // LANES):
            u_ref[layer, first_tile + k, HALO:HALO + seg, :] = u[:, k * LANES:(k + 1) * LANES]

    def conv(first_col):
        outs = []
        for j in range(first_col // LANES, (first_col + quad) // LANES):
            cols = slice(j * LANES, (j + 1) * LANES)
            acc = row_ref[layer, 4:5, cols]
            for tap in range(4):
                acc = acc + u_ref[layer, j, HALO - 3 + tap:HALO - 3 + tap + seg, :] * row_ref[layer, tap:tap + 1, cols]
            outs.append((acc + acc * jnp.tanh(acc)).astype(jnp.bfloat16))
        return outs

    dt_raw = round_bf16(dot(h, w_dt_ref[layer]))
    delta = softplus(dt_raw + row_ref[layer, 5:6, 0:LANES]).astype(jnp.bfloat16)
    project(d_inner)
    project(0)
    b_act, c_act = conv(d_inner)

    causal = lax.broadcasted_iota(jnp.int32, (sub, sub), 0) >= lax.broadcasted_iota(jnp.int32, (sub, sub), 1)
    tri = jnp.where(causal, 1.0, 0.0).astype(jnp.bfloat16)
    b_t = jnp.transpose(b_act.astype(jnp.float32)).astype(jnp.bfloat16)
    subs = [slice(i * sub, (i + 1) * sub) for i in range(seg // sub)]
    cums = [dot(tri, delta[rows]) * row_ref[layer, 6:7, 0:LANES] for rows in subs]
    cums_t = [jnp.transpose(cum) for cum in cums]
    scores = [jnp.where(causal, lax.dot_general(c_act[rows], b_act[rows], (((1,), (1,)), ((), ())), preferred_element_type=jnp.float32), 0.0) for rows in subs]

    sum_sq = [jnp.zeros((sub, LANES), jnp.float32) for _ in subs]
    quads = d_inner // quad
    for q in range(quads):
        cols = slice(q * quad, (q + 1) * quad)
        x_tiles = conv(q * quad)
        if q + 1 < quads:
            project((q + 1) * quad)
        z = dot(h, w_in_ref[layer, :, cols]).astype(jnp.bfloat16)
        dt_wide = dot(delta, expand_ref[:, cols])
        state = s_ref[layer, :, cols]
        for i, rows in enumerate(subs):
            y_inter = dot(c_act[rows], state.astype(jnp.bfloat16))
            x_ends = []
            decays = []
            for k in range(quad // LANES):
                lanes = slice(k * LANES, (k + 1) * LANES)
                head = (q * quad + k * LANES) // head_dim
                x_float = x_tiles[k][rows].astype(jnp.float32)
                x_scaled = x_float * dt_wide[rows, lanes]
                x_dot = x_scaled.astype(jnp.bfloat16)
                wide = [jnp.broadcast_to(cums[i][:, head + n:head + n + 1], (sub, LANES)) for n in range(2)]
                mix = [(jnp.exp2(jnp.minimum(wide[n] - cums_t[i][head + n:head + n + 1, :], 0.0)) * scores[i]).astype(jnp.bfloat16) for n in range(2)]
                none = jnp.zeros_like(x_dot)
                pair_rhs = jnp.concatenate([jnp.where(left, x_dot, none), jnp.where(left, none, x_dot)], axis=0)
                y_intra = dot(jnp.concatenate(mix, axis=1), pair_rhs)
                cum_pair = jnp.where(left, wide[0], wide[1])
                last = cum_pair[sub - 1:sub, :]
                x_ends.append((x_scaled * jnp.exp2(last - cum_pair)).astype(jnp.bfloat16))
                decays.append(jnp.exp2(last))
                tile = slice(q * quad + k * LANES, q * quad + (k + 1) * LANES)
                y = y_intra + y_inter[:, lanes] * jnp.exp2(cum_pair) + row_ref[layer, 7:8, tile] * x_float
                z_half = 0.5 * z[rows, lanes].astype(jnp.float32)
                gated = round_bf16(y) * (z_half + z_half * jnp.tanh(z_half))
                g_ref[rows, tile] = gated
                sum_sq[i] = sum_sq[i] + gated * gated
            state = state * jnp.concatenate(decays, axis=1) + dot(b_t[:, rows], jnp.concatenate(x_ends, axis=1))
        s_ref[layer, :, cols] = state

    for i, rows in enumerate(subs):
        scale = lax.rsqrt(jnp.sum(sum_sq[i], axis=-1, keepdims=True) * (1.0 / d_inner) + EPSILON)
        normed = (g_ref[rows, :] * scale * gate_ref[layer]).astype(jnp.bfloat16)
        seg_ref[piece, chunk, rows, :] = resid[rows] + dot(normed, w_out_ref[layer])

    @pl.when((layer == 1) & (chunk == me))
    def _():
        local_out(piece).start()

    @pl.when((layer == 1) & (chunk != me))
    def _():
        send_out(piece, chunk).start()

    @pl.when((chunk == chunks - 1) & (piece > 0))
    def _():
        local_state(piece - 1, layer).wait()
        for k in range(1, chunks):
            send_state(piece - 1, layer, lax.rem(me + k, chunks)).wait_send()

    @pl.when(chunk == chunks - 1)
    def _():
        for j in range(tiles):
            for k in range(3):
                row = k * 2 * 16 + j
                tail_f_ref[pl.ds(layer * 16 + row, 1), :] = u_ref[layer, j, seg + HALO - 3 + k:seg + HALO - 2 + k, :]

        @pl.when(layer == 1)
        def _():
            tail_ref[piece] = tail_f_ref[...].astype(jnp.bfloat16)
            local_tail(piece).start()
            for k in range(1, chunks):
                send_tail(piece, lax.rem(me + k, chunks)).start()

        per_device = d_inner // chunks
        final = jnp.transpose(s_ref[layer])
        for k in range(chunks):
            stage_ref[layer, k] = final[k * per_device:(k + 1) * per_device, :]
        local_state(piece, layer).start()
        for k in range(1, chunks):
            send_state(piece, layer, lax.rem(me + k, chunks)).start()

    @pl.when((piece == pieces - 1) & (chunk == chunks - 1) & (layer == 1))
    def _():
        for l in range(2):
            local_state(pieces - 1, l).wait()
        for p in range(pieces):
            local_out(p).wait()
            local_tail(p).wait()
            for k in range(1, chunks):
                peer = lax.rem(me + k, chunks)
                send_in(p, peer).wait_send()
                send_out(p, peer).wait_send()
                arrive_out(p, peer).wait_recv()
                send_tail(p, peer).wait_send()
                arrive_tail(p, peer).wait_recv()
                for l in range(2):
                    arrive_state(p, l, peer).wait_recv()
                    if p == pieces - 1:
                        send_state(p, l, peer).wait_send()


def solution(mesh):
    seg_count = mesh.shape['sp']

    def forward(resid, pre_norm, w_in, conv_w, conv_b, dt_bias, a_log, d_skip, gate_norm, w_out):
        batch, seg, d_model = resid.shape
        layers, d_inner, _ = w_out.shape
        heads = dt_bias.shape[1]
        head_dim = d_inner // heads
        conv_dim = conv_b.shape[1]
        d_state = (conv_dim - d_inner) // 2
        tiles = conv_dim // LANES
        pieces = batch // seg_count
        per_device = d_inner // seg_count
        params = (pre_norm, jnp.swapaxes(conv_w, 1, 2), conv_b, dt_bias, a_log, d_skip, gate_norm)

        def whole(a):
            return pl.BlockSpec(a.shape, lambda p, c, l: (0,) * a.ndim, pipeline_mode=pl.Buffered(1))

        hbm = pl.BlockSpec(memory_space=pl.ANY)
        out, state, tail = pl.pallas_call(
            functools.partial(forward_kernel, (d_inner, heads, seg, seg_count, pieces)),
            grid=(pieces, seg_count, layers),
            out_shape=(jax.ShapeDtypeStruct((batch, seg, d_model), jnp.float32),
                       jax.ShapeDtypeStruct((batch, layers, per_device, d_state), jnp.float32),
                       jax.ShapeDtypeStruct((batch, 6 * 16, LANES), jnp.bfloat16)),
            in_specs=[hbm, hbm, hbm] + [whole(a) for a in params],
            out_specs=(hbm, hbm, hbm),
            scratch_shapes=[pltpu.VMEM((pieces, seg_count, seg, d_model), jnp.float32),
                            pltpu.VMEM((layers, d_model, d_inner + conv_dim), jnp.bfloat16),
                            pltpu.VMEM((layers, d_model, LANES), jnp.bfloat16),
                            pltpu.VMEM(w_out.shape, jnp.bfloat16),
                            pltpu.VMEM((2, 256, d_model), jnp.bfloat16),
                            pltpu.VMEM((layers, 8, conv_dim), jnp.float32),
                            pltpu.VMEM((LANES, d_inner), jnp.bfloat16),
                            pltpu.VMEM((layers, tiles, HALO + seg, LANES), jnp.float32),
                            pltpu.VMEM((layers, d_state, d_inner), jnp.float32),
                            pltpu.VMEM((seg, d_inner), jnp.float32),
                            pltpu.VMEM((layers, seg_count, per_device, d_state), jnp.float32),
                            pltpu.VMEM((6 * 16, LANES), jnp.float32),
                            pltpu.VMEM((pieces, 6 * 16, LANES), jnp.bfloat16),
                            pltpu.SemaphoreType.DMA((layers,)),
                            pltpu.SemaphoreType.DMA((2,)),
                            pltpu.SemaphoreType.DMA((pieces, seg_count)),
                            pltpu.SemaphoreType.DMA((pieces, seg_count)),
                            pltpu.SemaphoreType.DMA((pieces, seg_count)),
                            pltpu.SemaphoreType.DMA((pieces, seg_count)),
                            pltpu.SemaphoreType.DMA((layers, seg_count)),
                            pltpu.SemaphoreType.DMA((pieces, layers, seg_count)),
                            pltpu.SemaphoreType.DMA((pieces, seg_count)),
                            pltpu.SemaphoreType.DMA((pieces, seg_count))],
            compiler_params=pltpu.CompilerParams(dimension_semantics=('arbitrary',) * 3, vmem_limit_bytes=67043328, collective_id=0, has_side_effects=True),
        )(resid, jnp.swapaxes(w_in, 1, 2), w_out, *params)
        tails = tail.reshape(batch, 3, layers, 16, LANES)[:, :, :, :tiles].reshape(batch, 3, layers, conv_dim)
        return out, state.reshape(batch, layers, heads // seg_count, head_dim, d_state), jnp.transpose(tails, (0, 2, 3, 1))

    return jax.shard_map(forward, mesh=mesh, in_specs=(P('dp', 'sp', None), P(), P(), P(), P(), P(), P(), P(), P(), P()), out_specs=(P('dp', 'sp', None), P('dp', None, 'sp', None, None), P('dp', None, None, None)), check_vma=False)
```

time: 704 us -> 650 us (0.923)
  blocking collectives: 39.2 us -> 0 us
  local copies, waits for them, and re-layouts: 44.4 us -> 23.8 us
    all_gather x1 -> x0, blocking collectives: 39.2 us -> none  [forward(): lax.all_gather(tails, 'sp', axis=1).reshape(batch, layers, conv_dim, 3)]
    unnamed x8 -> x7, local copies, waits for them, and re-layouts: 35.4 us -> 21.7 us
    pallas_call x1, Pallas kernels: 618 us -> 625 us  [forward(): pl.pallas_call(functools.partial(forward_kernel, (d_inner, heads, seg, se...]
where the time goes in v3:
time: 650 us; the launch traced here: 649 us
  Pallas kernels  625 us (96%)
  local copies, waits for them, and re-layouts  23.8 us (4%)
    pallas_call x1, Pallas kernels, forward(): pl.pallas_call(functools.partial(forward_kernel, (d_inner, heads, seg, se...  625 us
    unnamed x7, local copies, waits for them, and re-layouts  21.7 us

profile of v3, /device:TPU:0, one launch (start us, length us, event | category | flops | bytes accessed | tf_op | source)
XLA Modules:
  0.0 649.0 jit_solution(3037358367343692991)
XLA Ops:
  0.6 624.6 %shard_map.121 = (f32[32,256,768]{2,1,0:T(8,128)}, f32[32,2,192,128]{3,2,1,0:T(8,128)}, bf16[32,96,128]{2,1,0:T(8,128)(2,1)}) custom-call(f32[32,256,768]{2,1,0:T(8,128)} %x_hbm.1, bf16[2,3352,768]{2,1,0:T(8,128)(2,1)} %bitcast.8, bf16[2,1536,768]{2,1,0:T(8,128)(2,1)} %w_out_hbm.1, f32[2,768]{1,0:T(2,128)} %pre_ref.1, f32[2,4,1792]{2,1,0:T(4,128)} %bitcast.14, ...), custom_call_target="tpu_custom_call" | custom-call | tf_op jit(solution)/shard_map/pallas_call | solution.py:320
  625.2 2.0 reshape.18
  627.2 0.1 copy.18
  627.3 0.0 slice-start
  627.3 1.6 copy.14
  628.8 0.0 slice-start.1
  628.8 17.4 %copy.21 = f32[32,256,768]{2,1,0:T(8,128)} copy(f32[32,256,768]{2,1,0:T(8,128)} %get-tuple-element.15) | data formatting | bytes 50331648
  646.3 0.0 slice-done
  646.3 0.0 slice-done.1
  646.3 2.7 copy.22
  (1 shorter events, 0.0 us)
Async XLA Ops:
  627.3 19.0 %slice-start = ((s8[6291456]{0:T(1024)(128)(4,1)}), s8[4194304]{0:T(1024)(128)(4,1)S(1)}, s32[]{:S(2)}) async-start(s8[6291456]{0:T(1024)(128)(4,1)} %bitcast.9), calls=%async_computation | async-start | bytes 8388608
  628.8 17.5 %slice-start.1 = ((s8[6291456]{0:T(1024)(128)(4,1)}), s8[2097152]{0:T(1024)(128)(4,1)S(1)}, s32[]{:S(2)}) async-start(s8[6291456]{0:T(1024)(128)(4,1)} %bitcast.9), calls=%async_computation.1 | async-start | bytes 4194304

commit v4 on v3

v4 whole, which is shorter than its diff:
```python
import functools

import jax
import jax.numpy as jnp
from jax import lax
from jax.experimental import pallas as pl
from jax.experimental.pallas import tpu as pltpu
from jax.sharding import PartitionSpec as P

EPSILON = 1e-5
HALO = 8
SLOTS = 4
LANES = 128
LOG2_E = 1.4426950408889634


def softplus(v):
    return jnp.maximum(v, 0.0) + jnp.log1p(jnp.exp(-jnp.abs(v)))


def round_bf16(v):
    return v.astype(jnp.bfloat16).astype(jnp.float32)


def dot(a, b):
    return jnp.dot(a, b, preferred_element_type=jnp.float32)


def forward_kernel(dims, x_ref, w_in_hbm, w_out_hbm, pre_ref, conv_w_ref, conv_b_ref, dt_bias_ref, a_log_ref, d_skip_ref, gate_ref,
                   out_ref, state_hbm, tail_hbm,
                   res_ref, w_in_ref, w_dt_ref, w_out_ref, raw_ref, row_ref, expand_ref, u_ref, s_in_ref, s_out_ref, halo_in_ref, halo_out_ref, halo_f_ref, g_ref,
                   stage_ref, tail_f_ref, tail_ref,
                   w_sem, raw_sem, s_send, s_recv, halo_send, halo_recv, stage_send, stage_recv, tail_send, tail_recv, credit):
    d_inner, heads, seg, devices, batch = dims
    head_dim = d_inner // heads
    conv_dim = conv_b_ref.shape[1]
    tiles = conv_dim // LANES
    prompt = pl.program_id(0)
    layer = pl.program_id(1)
    me = lax.axis_index('sp')
    quad = 256
    sub = LANES
    quads = d_inner // quad
    bc = quads
    groups = ((bc, 0), (1, 2), (3, 4), (5,))
    spot = {b: (n, 6 * i) for n, group in enumerate(groups) for i, b in enumerate(group)}
    blocks = (d_inner + conv_dim) // quad
    steps = batch * 2
    step = prompt * 2 + layer
    slots = s_in_ref.shape[0]
    slot = lax.rem(step, slots)
    last_device = devices - 1
    after = lax.rem(me + 1, devices)
    before = lax.rem(me + devices - 1, devices)
    tail_group = batch // tail_send.shape[0]
    per_device = d_inner // devices

    def raw_copy(l, j, n):
        rows = pl.ds(pl.multiple_of(j * quad, quad), quad)
        return pltpu.make_async_copy(w_in_hbm.at[l, rows, :], raw_ref.at[n], raw_sem.at[n])

    def raw_dt_copy(l):
        return pltpu.make_async_copy(w_in_hbm.at[l, pl.ds(d_inner + conv_dim, heads), :], raw_ref.at[0, pl.ds(0, heads), :], raw_sem.at[0])

    def w_out_copy(l):
        return pltpu.make_async_copy(w_out_hbm.at[l], w_out_ref.at[l], w_sem.at[l])

    def remote(src, dst, send, recv, peer):
        return pltpu.make_async_remote_copy(src_ref=src, dst_ref=dst, send_sem=send, recv_sem=recv, device_id={'sp': peer},
                                            device_id_type=pl.DeviceIdType.MESH)

    def state_copy(n, q, peer):
        cols = pl.ds(q * quad, quad)
        return remote(s_out_ref.at[n, :, cols], s_in_ref.at[n, :, cols], s_send.at[n, q], s_recv.at[n, q], peer)

    def halo_copy(n, group, peer):
        return remote(halo_out_ref.at[n, group], halo_in_ref.at[n, group], halo_send.at[n, group], halo_recv.at[n, group], peer)

    def stage_copy(n, p, l, peer):
        return remote(stage_ref.at[n, peer], state_hbm.at[p, l], stage_send.at[n, peer], stage_recv, peer)

    def stage_local(n, p, l):
        return pltpu.make_async_copy(stage_ref.at[n, me], state_hbm.at[p, l], stage_send.at[n, me])

    def tail_copy(group, peer):
        rows = pl.ds(group * tail_group, tail_group)
        return remote(tail_ref.at[rows], tail_hbm.at[rows], tail_send.at[group, peer], tail_recv, peer)

    def tail_local(group):
        rows = pl.ds(group * tail_group, tail_group)
        return pltpu.make_async_copy(tail_ref.at[rows], tail_hbm.at[rows], tail_send.at[group, me])

    left = lax.broadcasted_iota(jnp.int32, (sub, LANES), 1) < head_dim

    @pl.when(step == 0)
    def _():
        for l in range(2):
            w_out_copy(l).start()
        barrier = pltpu.get_barrier_semaphore()
        for k in range(1, devices):
            pl.semaphore_signal(barrier, inc=1, device_id={'sp': lax.rem(me + k, devices)}, device_id_type=pl.DeviceIdType.MESH)

        tail_f_ref[...] = jnp.zeros(tail_f_ref.shape, jnp.float32)
        halo_f_ref[...] = jnp.zeros(halo_f_ref.shape, jnp.float32)
        row_ref[...] = jnp.zeros(row_ref.shape, jnp.float32)

        @pl.when(me == 0)
        def _():
            s_in_ref[...] = jnp.zeros(s_in_ref.shape, jnp.float32)
            halo_in_ref[...] = jnp.zeros(halo_in_ref.shape, jnp.bfloat16)

        for l in range(2):
            for tap in range(4):
                row_ref[l, tap:tap + 1, 0:conv_dim] = 0.5 * conv_w_ref[l, tap:tap + 1, :]
            row_ref[l, 4:5, 0:conv_dim] = 0.5 * conv_b_ref[l:l + 1, :]
            row_ref[l, 5:6, 0:heads] = dt_bias_ref[l:l + 1, :]
            row_ref[l, 6:7, 0:heads] = -jnp.exp(a_log_ref[l:l + 1, :]) * LOG2_E
            for k in range(d_inner // LANES):
                d_left = jnp.broadcast_to(d_skip_ref[l:l + 1, 2 * k:2 * k + 1], (1, LANES))
                d_right = jnp.broadcast_to(d_skip_ref[l:l + 1, 2 * k + 1:2 * k + 2], (1, LANES))
                row_ref[l, 7:8, k * LANES:(k + 1) * LANES] = jnp.where(left[0:1], d_left, d_right)
        lane_head = lax.shift_right_logical(lax.broadcasted_iota(jnp.int32, expand_ref.shape, 1), 6)
        expand_ref[...] = jnp.where(lax.broadcasted_iota(jnp.int32, expand_ref.shape, 0) == lane_head, 1.0, 0.0).astype(jnp.bfloat16)

        pl.semaphore_wait(barrier, devices - 1)

    @pl.when(prompt == 0)
    def _():
        for j in range(2):
            raw_copy(layer, j, j).start()

        @pl.loop(0, blocks)
        def _(j):
            n = lax.rem(j, 2)
            raw_copy(layer, j, n).wait()
            w_in_ref[layer, :, pl.ds(pl.multiple_of(j * quad, quad), quad)] = jnp.transpose(raw_ref[n])

            @pl.when(j + 2 < blocks)
            def _():
                raw_copy(layer, j + 2, n).start()

        raw_ref[0, 0:LANES, :] = jnp.zeros((LANES, raw_ref.shape[2]), jnp.bfloat16)
        raw_dt_copy(layer).start()
        raw_dt_copy(layer).wait()
        w_dt_ref[layer] = jnp.transpose(raw_ref[0, 0:LANES, :])
        w_out_copy(layer).wait()

    @pl.when((me < last_device) & (step >= slots))
    def _():
        for n in range(len(groups)):
            halo_copy(slot, n, after).wait_send()
        for q in range(quads):
            state_copy(slot, q, after).wait_send()
        pl.semaphore_wait(credit, 1)

    @pl.when(layer == 0)
    def _():
        res_ref[...] = x_ref[0]

    resid = res_ref[...]
    mean_sq = jnp.mean(resid * resid, axis=-1, keepdims=True)
    h = (resid * lax.rsqrt(mean_sq + EPSILON) * pre_ref[pl.ds(layer, 1), :]).astype(jnp.bfloat16)

    def project(b):
        first_col = b * quad
        u = round_bf16(dot(h, w_in_ref[layer, :, d_inner + first_col:d_inner + first_col + quad]))
        for k in range(quad // LANES):
            j = first_col // LANES + k
            lanes = slice(k * LANES, (k + 1) * LANES)
            u_ref[j, HALO:HALO + seg, :] = u[:, lanes]
            group, first = spot[b]
            for tap in range(3):
                row = first + 2 * tap + k
                halo_f_ref[0, group, row:row + 1, :] = u_ref[j, HALO + seg - 3 + tap:HALO + seg - 2 + tap, :]

    def project_group(group):
        for b in groups[group]:
            project(b)
        halo_out_ref[slot, group] = halo_f_ref[0, group].astype(jnp.bfloat16)

    def take_halo(group):
        halo_f_ref[1, group] = halo_in_ref[slot, group].astype(jnp.float32)

    def conv(b):
        outs = []
        for j in range(b * quad // LANES, (b + 1) * quad // LANES):
            cols = slice(j * LANES, (j + 1) * LANES)
            group, first = spot[b]
            for tap in range(3):
                row = first + 2 * tap + j % 2
                u_ref[j, HALO - 3 + tap:HALO - 2 + tap, :] = halo_f_ref[1, group, row:row + 1, :]
            acc = row_ref[layer, 4:5, cols]
            for tap in range(4):
                acc = acc + u_ref[j, HALO - 3 + tap:HALO - 3 + tap + seg, :] * row_ref[layer, tap:tap + 1, cols]
            outs.append((acc + acc * jnp.tanh(acc)).astype(jnp.bfloat16))
        return outs

    dt_raw = round_bf16(dot(h, w_dt_ref[layer]))
    delta = softplus(dt_raw + row_ref[layer, 5:6, 0:LANES]).astype(jnp.bfloat16)
    project_group(0)

    @pl.when(me < last_device)
    def _():
        halo_copy(slot, 0, after).start()

    @pl.when(me > 0)
    def _():
        halo_copy(slot, 0, before).wait_recv()
        state_copy(slot, 0, before).wait_recv()

    take_halo(0)
    b_act, c_act = conv(bc)
    causal = lax.broadcasted_iota(jnp.int32, (sub, sub), 0) >= lax.broadcasted_iota(jnp.int32, (sub, sub), 1)
    tri = jnp.where(causal, 1.0, 0.0).astype(jnp.bfloat16)
    b_t = jnp.transpose(b_act.astype(jnp.float32)).astype(jnp.bfloat16)
    subs = [slice(i * sub, (i + 1) * sub) for i in range(seg // sub)]
    cums = [dot(tri, delta[rows]) * row_ref[layer, 6:7, 0:LANES] for rows in subs]
    cums_t = [jnp.transpose(cum) for cum in cums]
    scores = [jnp.where(causal, lax.dot_general(c_act[rows], b_act[rows], (((1,), (1,)), ((), ())), preferred_element_type=jnp.float32), 0.0) for rows in subs]

    sum_sq = [jnp.zeros((sub, LANES), jnp.float32) for _ in subs]
    for q in range(quads):
        cols = slice(q * quad, (q + 1) * quad)
        x_tiles = conv(q)
        if q + 1 < len(groups):
            project_group(q + 1)
        z = dot(h, w_in_ref[layer, :, cols]).astype(jnp.bfloat16)
        dt_wide = dot(delta, expand_ref[:, cols])
        state = s_in_ref[slot, :, cols]
        for i, rows in enumerate(subs):
            y_inter = dot(c_act[rows], state.astype(jnp.bfloat16))
            x_ends = []
            decays = []
            for k in range(quad // LANES):
                lanes = slice(k * LANES, (k + 1) * LANES)
                head = (q * quad + k * LANES) // head_dim
                x_float = x_tiles[k][rows].astype(jnp.float32)
                x_scaled = x_float * dt_wide[rows, lanes]
                x_dot = x_scaled.astype(jnp.bfloat16)
                wide = [jnp.broadcast_to(cums[i][:, head + n:head + n + 1], (sub, LANES)) for n in range(2)]
                mix = [(jnp.exp2(jnp.minimum(wide[n] - cums_t[i][head + n:head + n + 1, :], 0.0)) * scores[i]).astype(jnp.bfloat16) for n in range(2)]
                none = jnp.zeros_like(x_dot)
                pair_rhs = jnp.concatenate([jnp.where(left, x_dot, none), jnp.where(left, none, x_dot)], axis=0)
                y_intra = dot(jnp.concatenate(mix, axis=1), pair_rhs)
                cum_pair = jnp.where(left, wide[0], wide[1])
                last = cum_pair[sub - 1:sub, :]
                x_ends.append((x_scaled * jnp.exp2(last - cum_pair)).astype(jnp.bfloat16))
                decays.append(jnp.exp2(last))
                tile = slice(q * quad + k * LANES, q * quad + (k + 1) * LANES)
                y = y_intra + y_inter[:, lanes] * jnp.exp2(cum_pair) + row_ref[layer, 7:8, tile] * x_float
                z_half = 0.5 * z[rows, lanes].astype(jnp.float32)
                gated = round_bf16(y) * (z_half + z_half * jnp.tanh(z_half))
                g_ref[rows, tile] = gated
                sum_sq[i] = sum_sq[i] + gated * gated
            state = state * jnp.concatenate(decays, axis=1) + dot(b_t[:, rows], jnp.concatenate(x_ends, axis=1))
        s_out_ref[slot, :, cols] = state

        @pl.when(me < last_device)
        def _():
            state_copy(slot, q, after).start()
            if q + 1 < len(groups):
                halo_copy(slot, q + 1, after).start()

        if q + 1 < quads:
            @pl.when(me > 0)
            def _():
                if spot[q + 1][1] == 0:
                    halo_copy(slot, spot[q + 1][0], before).wait_recv()
                state_copy(slot, q + 1, before).wait_recv()

            if spot[q + 1][1] == 0:
                take_halo(spot[q + 1][0])

    @pl.when((me > 0) & (step < steps - slots))
    def _():
        pl.semaphore_signal(credit, inc=1, device_id={'sp': before}, device_id_type=pl.DeviceIdType.MESH)

    @pl.when(me == last_device)
    def _():
        n = lax.rem(step, 2)

        @pl.when(step >= 2)
        def _():
            stage_local(n, prompt - 1, layer).wait()
            for k in range(1, devices):
                stage_copy(n, prompt - 1, layer, lax.rem(me + k, devices)).wait_send()

        final = jnp.transpose(s_out_ref[slot])
        for k in range(devices):
            stage_ref[n, k] = final[k * per_device:(k + 1) * per_device, :]
        stage_local(n, prompt, layer).start()
        for k in range(1, devices):
            stage_copy(n, prompt, layer, lax.rem(me + k, devices)).start()

        for j in range(tiles):
            for k in range(3):
                row = k * 2 * 16 + j
                tail_f_ref[pl.ds(layer * 16 + row, 1), :] = u_ref[j, seg + HALO - 3 + k:seg + HALO - 2 + k, :]

        @pl.when(layer == 1)
        def _():
            tail_ref[prompt] = tail_f_ref[...].astype(jnp.bfloat16)

        @pl.when((layer == 1) & (lax.rem(prompt, tail_group) == tail_group - 1))
        def _():
            group = lax.div(prompt, tail_group)
            tail_local(group).start()
            for k in range(1, devices):
                tail_copy(group, lax.rem(me + k, devices)).start()

    for i, rows in enumerate(subs):
        scale = lax.rsqrt(jnp.sum(sum_sq[i], axis=-1, keepdims=True) * (1.0 / d_inner) + EPSILON)
        normed = (g_ref[rows, :] * scale * gate_ref[layer]).astype(jnp.bfloat16)
        res_ref[rows, :] = resid[rows] + dot(normed, w_out_ref[layer])

    @pl.when(layer == 1)
    def _():
        out_ref[0] = res_ref[...]

    @pl.when(step == steps - 1)
    def _():
        @pl.when(me < last_device)
        def _():
            for n in range(slots):
                for group in range(len(groups)):
                    halo_copy(n, group, after).wait_send()
                for q in range(quads):
                    state_copy(n, q, after).wait_send()
            pltpu.make_async_copy(state_hbm, state_hbm, stage_recv).wait()
            pltpu.make_async_copy(tail_hbm, tail_hbm, tail_recv).wait()

        @pl.when(me == last_device)
        def _():
            for n in range(2):
                stage_local(n, batch - 1, n).wait()
                for k in range(1, devices):
                    stage_copy(n, batch - 1, n, lax.rem(me + k, devices)).wait_send()
            for group in range(tail_send.shape[0]):
                tail_local(group).wait()
                for k in range(1, devices):
                    tail_copy(group, lax.rem(me + k, devices)).wait_send()


def solution(mesh):
    seg_count = mesh.shape['sp']

    def forward(resid, pre_norm, w_in, conv_w, conv_b, dt_bias, a_log, d_skip, gate_norm, w_out):
        batch, seg, d_model = resid.shape
        layers, d_inner, _ = w_out.shape
        heads = dt_bias.shape[1]
        head_dim = d_inner // heads
        conv_dim = conv_b.shape[1]
        d_state = (conv_dim - d_inner) // 2
        tiles = conv_dim // LANES
        per_device = d_inner // seg_count
        quads = d_inner // 256
        params = (pre_norm, jnp.swapaxes(conv_w, 1, 2), conv_b, dt_bias, a_log, d_skip, gate_norm)

        def whole(a):
            return pl.BlockSpec(a.shape, lambda p, l: (0,) * a.ndim, pipeline_mode=pl.Buffered(1))

        hbm = pl.BlockSpec(memory_space=pl.ANY)
        block = pl.BlockSpec((1, seg, d_model), lambda p, l: (p, 0, 0))
        out, state, tail = pl.pallas_call(
            functools.partial(forward_kernel, (d_inner, heads, seg, seg_count, batch)),
            grid=(batch, layers),
            out_shape=(jax.ShapeDtypeStruct((batch, seg, d_model), jnp.float32),
                       jax.ShapeDtypeStruct((batch, layers, per_device, d_state), jnp.float32),
                       jax.ShapeDtypeStruct((batch, 6 * 16, LANES), jnp.bfloat16)),
            in_specs=[block, hbm, hbm] + [whole(a) for a in params],
            out_specs=(block, hbm, hbm),
            scratch_shapes=[pltpu.VMEM((seg, d_model), jnp.float32),
                            pltpu.VMEM((layers, d_model, d_inner + conv_dim), jnp.bfloat16),
                            pltpu.VMEM((layers, d_model, LANES), jnp.bfloat16),
                            pltpu.VMEM(w_out.shape, jnp.bfloat16),
                            pltpu.VMEM((2, 256, d_model), jnp.bfloat16),
                            pltpu.VMEM((layers, 8, conv_dim), jnp.float32),
                            pltpu.VMEM((LANES, d_inner), jnp.bfloat16),
                            pltpu.VMEM((tiles, HALO + seg, LANES), jnp.float32),
                            pltpu.VMEM((SLOTS, d_state, d_inner), jnp.float32),
                            pltpu.VMEM((SLOTS, d_state, d_inner), jnp.float32),
                            pltpu.VMEM((SLOTS, 4, 16, LANES), jnp.bfloat16),
                            pltpu.VMEM((SLOTS, 4, 16, LANES), jnp.bfloat16),
                            pltpu.VMEM((2, 4, 16, LANES), jnp.float32),
                            pltpu.VMEM((seg, d_inner), jnp.float32),
                            pltpu.VMEM((2, seg_count, per_device, d_state), jnp.float32),
                            pltpu.VMEM((6 * 16, LANES), jnp.float32),
                            pltpu.VMEM((batch, 6 * 16, LANES), jnp.bfloat16),
                            pltpu.SemaphoreType.DMA((layers,)),
                            pltpu.SemaphoreType.DMA((2,)),
                            pltpu.SemaphoreType.DMA((SLOTS, quads)),
                            pltpu.SemaphoreType.DMA((SLOTS, quads)),
                            pltpu.SemaphoreType.DMA((SLOTS, 4)),
                            pltpu.SemaphoreType.DMA((SLOTS, 4)),
                            pltpu.SemaphoreType.DMA((2, seg_count)),
                            pltpu.SemaphoreType.DMA,
                            pltpu.SemaphoreType.DMA((8, seg_count)),
                            pltpu.SemaphoreType.DMA,
                            pltpu.SemaphoreType.REGULAR],
            compiler_params=pltpu.CompilerParams(dimension_semantics=('arbitrary',) * 2, vmem_limit_bytes=67043328, collective_id=0, has_side_effects=True),
        )(resid, jnp.swapaxes(w_in, 1, 2), w_out, *params)
        tails = tail.reshape(batch, 3, layers, 16, LANES)[:, :, :, :tiles].reshape(batch, 3, layers, conv_dim)
        return out, state.reshape(batch, layers, heads // seg_count, head_dim, d_state), jnp.transpose(tails, (0, 2, 3, 1))

    return jax.shard_map(forward, mesh=mesh, in_specs=(P('dp', 'sp', None), P(), P(), P(), P(), P(), P(), P(), P(), P()), out_specs=(P('dp', 'sp', None), P('dp', None, 'sp', None, None), P('dp', None, None, None)), check_vma=False)
```

time: 650 us -> 633 us (0.974)
  Pallas kernels: 625 us -> 607 us
    pallas_call x1, Pallas kernels: 625 us -> 607 us  [forward(): pl.pallas_call(functools.partial(forward_kernel, (d_inner, heads, seg, se...]
where the time goes in v4:
time: 633 us; the launch traced here: 632 us
  Pallas kernels  607 us (96%)
  local copies, waits for them, and re-layouts  23.8 us (4%)
    pallas_call x1, Pallas kernels, forward(): pl.pallas_call(functools.partial(forward_kernel, (d_inner, heads, seg, se...  607 us
    unnamed x7, local copies, waits for them, and re-layouts  21.7 us

profile of v4, /device:TPU:0, one launch (start us, length us, event | category | flops | bytes accessed | tf_op | source)
XLA Modules:
  0.0 631.9 jit_solution(7211954736763669631)
XLA Ops:
  0.6 607.4 %shard_map.121 = (f32[32,256,768]{2,1,0:T(8,128)}, f32[32,2,192,128]{3,2,1,0:T(8,128)}, bf16[32,96,128]{2,1,0:T(8,128)(2,1)}) custom-call(f32[32,256,768]{2,1,0:T(8,128)} %x_ref.1, bf16[2,3352,768]{2,1,0:T(8,128)(2,1)} %bitcast.8, bf16[2,1536,768]{2,1,0:T(8,128)(2,1)} %w_out_hbm.1, f32[2,768]{1,0:T(2,128)} %pre_ref.1, f32[2,4,1792]{2,1,0:T(4,128)} %bitcast.14, ...), custom_call_target="tpu_custom_call" | custom-call | tf_op jit(solution)/shard_map/pallas_call | solution.py:364
  608.1 2.0 reshape.18
  610.0 0.1 copy.18
  610.1 0.0 slice-start
  610.1 1.6 copy.14
  611.7 0.0 slice-start.1
  611.7 17.4 %copy.21 = f32[32,256,768]{2,1,0:T(8,128)} copy(f32[32,256,768]{2,1,0:T(8,128)} %get-tuple-element.15) | data formatting | bytes 50331648
  629.1 0.0 slice-done
  629.1 0.0 slice-done.1
  629.1 2.7 copy.22
  (1 shorter events, 0.0 us)
Async XLA Ops:
  610.1 19.0 %slice-start = ((s8[6291456]{0:T(1024)(128)(4,1)}), s8[4194304]{0:T(1024)(128)(4,1)S(1)}, s32[]{:S(2)}) async-start(s8[6291456]{0:T(1024)(128)(4,1)} %bitcast.9), calls=%async_computation | async-start | bytes 8388608
  611.7 17.5 %slice-start.1 = ((s8[6291456]{0:T(1024)(128)(4,1)}), s8[2097152]{0:T(1024)(128)(4,1)S(1)}, s32[]{:S(2)}) async-start(s8[6291456]{0:T(1024)(128)(4,1)} %bitcast.9), calls=%async_computation.1 | async-start | bytes 4194304

commit v5 on v4

--- a/solution.py
+++ b/solution.py
@@ -26,9 +26,13 @@
     return jnp.dot(a, b, preferred_element_type=jnp.float32)
 
 
+def dot_nt(a, b):
+    return lax.dot_general(a, b, (((1,), (1,)), ((), ())), preferred_element_type=jnp.float32)
+
+
 def forward_kernel(dims, x_ref, w_in_hbm, w_out_hbm, pre_ref, conv_w_ref, conv_b_ref, dt_bias_ref, a_log_ref, d_skip_ref, gate_ref,
                    out_ref, state_hbm, tail_hbm,
-                   res_ref, w_in_ref, w_dt_ref, w_out_ref, raw_ref, row_ref, expand_ref, u_ref, s_in_ref, s_out_ref, halo_in_ref, halo_out_ref, halo_f_ref, g_ref,
+                   res_ref, w_in_ref, w_out_ref, row_ref, expand_ref, u_ref, s_in_ref, s_out_ref, halo_in_ref, halo_out_ref, halo_f_ref, g_ref,
                    stage_ref, tail_f_ref, tail_ref,
                    w_sem, raw_sem, s_send, s_recv, halo_send, halo_recv, stage_send, stage_recv, tail_send, tail_recv, credit):
     d_inner, heads, seg, devices, batch = dims
@@ -44,7 +48,6 @@
     bc = quads
     groups = ((bc, 0), (1, 2), (3, 4), (5,))
     spot = {b: (n, 6 * i) for n, group in enumerate(groups) for i, b in enumerate(group)}
-    blocks = (d_inner + conv_dim) // quad
     steps = batch * 2
     step = prompt * 2 + layer
     slots = s_in_ref.shape[0]
@@ -55,12 +58,9 @@
     tail_group = batch // tail_send.shape[0]
     per_device = d_inner // devices
 
-    def raw_copy(l, j, n):
-        rows = pl.ds(pl.multiple_of(j * quad, quad), quad)
-        return pltpu.make_async_copy(w_in_hbm.at[l, rows, :], raw_ref.at[n], raw_sem.at[n])
-
-    def raw_dt_copy(l):
-        return pltpu.make_async_copy(w_in_hbm.at[l, pl.ds(d_inner + conv_dim, heads), :], raw_ref.at[0, pl.ds(0, heads), :], raw_sem.at[0])
+    def w_in_copy(l):
+        rows = pl.ds(0, w_in_hbm.shape[1])
+        return pltpu.make_async_copy(w_in_hbm.at[l], w_in_ref.at[l, rows, :], raw_sem.at[l])
 
     def w_out_copy(l):
         return pltpu.make_async_copy(w_out_hbm.at[l], w_out_ref.at[l], w_sem.at[l])
@@ -95,6 +95,7 @@
     @pl.when(step == 0)
     def _():
         for l in range(2):
+            w_in_copy(l).start()
             w_out_copy(l).start()
         barrier = pltpu.get_barrier_semaphore()
         for k in range(1, devices):
@@ -126,24 +127,9 @@
 
     @pl.when(prompt == 0)
     def _():
-        for j in range(2):
-            raw_copy(layer, j, j).start()
-
-        @pl.loop(0, blocks)
-        def _(j):
-            n = lax.rem(j, 2)
-            raw_copy(layer, j, n).wait()
-            w_in_ref[layer, :, pl.ds(pl.multiple_of(j * quad, quad), quad)] = jnp.transpose(raw_ref[n])
-
-            @pl.when(j + 2 < blocks)
-            def _():
-                raw_copy(layer, j + 2, n).start()
-
-        raw_ref[0, 0:LANES, :] = jnp.zeros((LANES, raw_ref.shape[2]), jnp.bfloat16)
-        raw_dt_copy(layer).start()
-        raw_dt_copy(layer).wait()
-        w_dt_ref[layer] = jnp.transpose(raw_ref[0, 0:LANES, :])
+        w_in_copy(layer).wait()
         w_out_copy(layer).wait()
+        w_in_ref[layer, w_in_hbm.shape[1]:, :] = jnp.zeros((w_in_ref.shape[1] - w_in_hbm.shape[1], w_in_ref.shape[2]), jnp.bfloat16)
 
     @pl.when((me < last_device) & (step >= slots))
     def _():
@@ -163,7 +149,7 @@
 
     def project(b):
         first_col = b * quad
-        u = round_bf16(dot(h, w_in_ref[layer, :, d_inner + first_col:d_inner + first_col + quad]))
+        u = round_bf16(dot_nt(h, w_in_ref[layer, d_inner + first_col:d_inner + first_col + quad, :]))
         for k in range(quad // LANES):
             j = first_col // LANES + k
             lanes = slice(k * LANES, (k + 1) * LANES)
@@ -195,7 +181,7 @@
             outs.append((acc + acc * jnp.tanh(acc)).astype(jnp.bfloat16))
         return outs
 
-    dt_raw = round_bf16(dot(h, w_dt_ref[layer]))
+    dt_raw = round_bf16(dot_nt(h, w_in_ref[layer, d_inner + conv_dim:d_inner + conv_dim + LANES, :]))
     delta = softplus(dt_raw + row_ref[layer, 5:6, 0:LANES]).astype(jnp.bfloat16)
     project_group(0)
 
@@ -206,7 +192,6 @@
     @pl.when(me > 0)
     def _():
         halo_copy(slot, 0, before).wait_recv()
-        state_copy(slot, 0, before).wait_recv()
 
     take_halo(0)
     b_act, c_act = conv(bc)
@@ -216,21 +201,21 @@
     subs = [slice(i * sub, (i + 1) * sub) for i in range(seg // sub)]
     cums = [dot(tri, delta[rows]) * row_ref[layer, 6:7, 0:LANES] for rows in subs]
     cums_t = [jnp.transpose(cum) for cum in cums]
-    scores = [jnp.where(causal, lax.dot_general(c_act[rows], b_act[rows], (((1,), (1,)), ((), ())), preferred_element_type=jnp.float32), 0.0) for rows in subs]
-
-    sum_sq = [jnp.zeros((sub, LANES), jnp.float32) for _ in subs]
-    for q in range(quads):
+    scores = [jnp.where(causal, dot_nt(c_act[rows], b_act[rows]), 0.0) for rows in subs]
+
+    def local_part(q):
         cols = slice(q * quad, (q + 1) * quad)
         x_tiles = conv(q)
         if q + 1 < len(groups):
             project_group(q + 1)
-        z = dot(h, w_in_ref[layer, :, cols]).astype(jnp.bfloat16)
+        z = dot_nt(h, w_in_ref[layer, cols, :]).astype(jnp.bfloat16)
         dt_wide = dot(delta, expand_ref[:, cols])
-        state = s_in_ref[slot, :, cols]
+        parts = []
         for i, rows in enumerate(subs):
-            y_inter = dot(c_act[rows], state.astype(jnp.bfloat16))
             x_ends = []
             decays = []
+            ys = []
+            scales = []
             for k in range(quad // LANES):
                 lanes = slice(k * LANES, (k + 1) * LANES)
                 head = (q * quad + k * LANES) // head_dim
@@ -247,29 +232,55 @@
                 x_ends.append((x_scaled * jnp.exp2(last - cum_pair)).astype(jnp.bfloat16))
                 decays.append(jnp.exp2(last))
                 tile = slice(q * quad + k * LANES, q * quad + (k + 1) * LANES)
-                y = y_intra + y_inter[:, lanes] * jnp.exp2(cum_pair) + row_ref[layer, 7:8, tile] * x_float
+                ys.append(y_intra + row_ref[layer, 7:8, tile] * x_float)
+                scales.append(jnp.exp2(cum_pair))
+            added = dot(b_t[:, rows], jnp.concatenate(x_ends, axis=1))
+            parts.append((jnp.concatenate(decays, axis=1), added, ys, scales))
+        return z, parts
+
+    def gate_part(q, z, parts, states, sums):
+        for i, rows in enumerate(subs):
+            y_inter = dot(c_act[rows], states[i].astype(jnp.bfloat16))
+            for k in range(quad // LANES):
+                lanes = slice(k * LANES, (k + 1) * LANES)
+                y = parts[i][2][k] + y_inter[:, lanes] * parts[i][3][k]
                 z_half = 0.5 * z[rows, lanes].astype(jnp.float32)
                 gated = round_bf16(y) * (z_half + z_half * jnp.tanh(z_half))
-                g_ref[rows, tile] = gated
-                sum_sq[i] = sum_sq[i] + gated * gated
-            state = state * jnp.concatenate(decays, axis=1) + dot(b_t[:, rows], jnp.concatenate(x_ends, axis=1))
-        s_out_ref[slot, :, cols] = state
+                g_ref[rows, q * quad + k * LANES:q * quad + (k + 1) * LANES] = gated
+                sums[i] = sums[i] + gated * gated
+
+    sum_sq = [jnp.zeros((sub, LANES), jnp.float32) for _ in subs]
+    z, parts = local_part(0)
+    for q in range(quads):
+        cols = slice(q * quad, (q + 1) * quad)
 
         @pl.when(me < last_device)
         def _():
-            state_copy(slot, q, after).start()
             if q + 1 < len(groups):
                 halo_copy(slot, q + 1, after).start()
 
-        if q + 1 < quads:
+        @pl.when(me > 0)
+        def _():
+            state_copy(slot, q, before).wait_recv()
+
+        states = [s_in_ref[slot, :, cols]]
+        for decay, added, _, _ in parts:
+            states.append(states[-1] * decay + added)
+        s_out_ref[slot, :, cols] = states[-1]
+
+        @pl.when(me < last_device)
+        def _():
+            state_copy(slot, q, after).start()
+
+        if q + 1 < quads and spot[q + 1][1] == 0:
             @pl.when(me > 0)
             def _():
-                if spot[q + 1][1] == 0:
-                    halo_copy(slot, spot[q + 1][0], before).wait_recv()
-                state_copy(slot, q + 1, before).wait_recv()
-
-            if spot[q + 1][1] == 0:
-                take_halo(spot[q + 1][0])
+                halo_copy(slot, spot[q + 1][0], before).wait_recv()
+
+            take_halo(spot[q + 1][0])
+        gate_part(q, z, parts, states, sum_sq)
+        if q + 1 < quads:
+            z, parts = local_part(q + 1)
 
     @pl.when((me > 0) & (step < steps - slots))
     def _():
@@ -370,10 +381,8 @@
             in_specs=[block, hbm, hbm] + [whole(a) for a in params],
             out_specs=(block, hbm, hbm),
             scratch_shapes=[pltpu.VMEM((seg, d_model), jnp.float32),
-                            pltpu.VMEM((layers, d_model, d_inner + conv_dim), jnp.bfloat16),
-                            pltpu.VMEM((layers, d_model, LANES), jnp.bfloat16),
+                            pltpu.VMEM((layers, d_inner + conv_dim + LANES, d_model), jnp.bfloat16),
                             pltpu.VMEM(w_out.shape, jnp.bfloat16),
-                            pltpu.VMEM((2, 256, d_model), jnp.bfloat16),
                             pltpu.VMEM((layers, 8, conv_dim), jnp.float32),
                             pltpu.VMEM((LANES, d_inner), jnp.bfloat16),
                             pltpu.VMEM((tiles, HALO + seg, LANES), jnp.float32),

time: 633 us -> 610 us (0.964)
  Pallas kernels: 607 us -> 585 us
    pallas_call x1, Pallas kernels: 607 us -> 585 us  [forward(): pl.pallas_call(functools.partial(forward_kernel, (d_inner, heads, seg, se...]
where the time goes in v5:
time: 610 us
  Pallas kernels  585 us (96%)
  local copies, waits for them, and re-layouts  23.8 us (4%)
    pallas_call x1, Pallas kernels, forward(): pl.pallas_call(functools.partial(forward_kernel, (d_inner, heads, seg, se...  585 us
    unnamed x7, local copies, waits for them, and re-layouts  21.7 us

profile of v5, /device:TPU:0, one launch (start us, length us, event | category | flops | bytes accessed | tf_op | source)
XLA Modules:
  0.0 609.6 jit_solution(1977863165491103133)
XLA Ops:
  0.6 585.2 %shard_map.121 = (f32[32,256,768]{2,1,0:T(8,128)}, f32[32,2,192,128]{3,2,1,0:T(8,128)}, bf16[32,96,128]{2,1,0:T(8,128)(2,1)}) custom-call(f32[32,256,768]{2,1,0:T(8,128)} %x_ref.1, bf16[2,3352,768]{2,1,0:T(8,128)(2,1)} %bitcast.8, bf16[2,1536,768]{2,1,0:T(8,128)(2,1)} %w_out_hbm.1, f32[2,768]{1,0:T(2,128)} %pre_ref.1, f32[2,4,1792]{2,1,0:T(4,128)} %bitcast.14, ...), custom_call_target="tpu_custom_call" | custom-call | tf_op jit(solution)/shard_map/pallas_call | solution.py:375
  585.8 2.0 reshape.18
  587.8 0.1 copy.18
  587.8 0.0 slice-start
  587.9 1.6 copy.14
  589.4 0.0 slice-start.1
  589.4 17.4 %copy.21 = f32[32,256,768]{2,1,0:T(8,128)} copy(f32[32,256,768]{2,1,0:T(8,128)} %get-tuple-element.15) | data formatting | bytes 50331648
  606.9 0.0 slice-done
  606.9 0.0 slice-done.1
  606.9 2.7 copy.22
  (1 shorter events, 0.0 us)
Async XLA Ops:
  587.8 19.0 %slice-start = ((s8[6291456]{0:T(1024)(128)(4,1)}), s8[4194304]{0:T(1024)(128)(4,1)S(1)}, s32[]{:S(2)}) async-start(s8[6291456]{0:T(1024)(128)(4,1)} %bitcast.9), calls=%async_computation | async-start | bytes 8388608
  589.4 17.5 %slice-start.1 = ((s8[6291456]{0:T(1024)(128)(4,1)}), s8[2097152]{0:T(1024)(128)(4,1)S(1)}, s32[]{:S(2)}) async-start(s8[6291456]{0:T(1024)(128)(4,1)} %bitcast.9), calls=%async_computation.1 | async-start | bytes 4194304

commit v6 on v5

--- a/solution.py
+++ b/solution.py
@@ -46,8 +46,9 @@
     sub = LANES
     quads = d_inner // quad
     bc = quads
-    groups = ((bc, 0), (1, 2), (3, 4), (5,))
-    spot = {b: (n, 6 * i) for n, group in enumerate(groups) for i, b in enumerate(group)}
+    groups = ((bc, 0), tuple(range(1, quads)))
+    spans = ((0, 16), (16, 32))
+    spot = {b: (n, spans[n][0] + 6 * i) for n, group in enumerate(groups) for i, b in enumerate(group)}
     steps = batch * 2
     step = prompt * 2 + layer
     slots = s_in_ref.shape[0]
@@ -74,7 +75,8 @@
         return remote(s_out_ref.at[n, :, cols], s_in_ref.at[n, :, cols], s_send.at[n, q], s_recv.at[n, q], peer)
 
     def halo_copy(n, group, peer):
-        return remote(halo_out_ref.at[n, group], halo_in_ref.at[n, group], halo_send.at[n, group], halo_recv.at[n, group], peer)
+        rows = pl.ds(*spans[group])
+        return remote(halo_out_ref.at[n, rows], halo_in_ref.at[n, rows], halo_send.at[n, group], halo_recv.at[n, group], peer)
 
     def stage_copy(n, p, l, peer):
         return remote(stage_ref.at[n, peer], state_hbm.at[p, l], stage_send.at[n, peer], stage_recv, peer)
@@ -157,15 +159,17 @@
             group, first = spot[b]
             for tap in range(3):
                 row = first + 2 * tap + k
-                halo_f_ref[0, group, row:row + 1, :] = u_ref[j, HALO + seg - 3 + tap:HALO + seg - 2 + tap, :]
+                halo_f_ref[0, row:row + 1, :] = u_ref[j, HALO + seg - 3 + tap:HALO + seg - 2 + tap, :]
 
     def project_group(group):
         for b in groups[group]:
             project(b)
-        halo_out_ref[slot, group] = halo_f_ref[0, group].astype(jnp.bfloat16)
+        first, count = spans[group]
+        halo_out_ref[slot, first:first + count, :] = halo_f_ref[0, first:first + count, :].astype(jnp.bfloat16)
 
     def take_halo(group):
-        halo_f_ref[1, group] = halo_in_ref[slot, group].astype(jnp.float32)
+        first, count = spans[group]
+        halo_f_ref[1, first:first + count, :] = halo_in_ref[slot, first:first + count, :].astype(jnp.float32)
 
     def conv(b):
         outs = []
@@ -174,7 +178,7 @@
             group, first = spot[b]
             for tap in range(3):
                 row = first + 2 * tap + j % 2
-                u_ref[j, HALO - 3 + tap:HALO - 2 + tap, :] = halo_f_ref[1, group, row:row + 1, :]
+                u_ref[j, HALO - 3 + tap:HALO - 2 + tap, :] = halo_f_ref[1, row:row + 1, :]
             acc = row_ref[layer, 4:5, cols]
             for tap in range(4):
                 acc = acc + u_ref[j, HALO - 3 + tap:HALO - 3 + tap + seg, :] * row_ref[layer, tap:tap + 1, cols]
@@ -272,12 +276,12 @@
         def _():
             state_copy(slot, q, after).start()
 
-        if q + 1 < quads and spot[q + 1][1] == 0:
+        if q == 0:
             @pl.when(me > 0)
             def _():
-                halo_copy(slot, spot[q + 1][0], before).wait_recv()
-
-            take_halo(spot[q + 1][0])
+                halo_copy(slot, 1, before).wait_recv()
+
+            take_halo(1)
         gate_part(q, z, parts, states, sum_sq)
         if q + 1 < quads:
             z, parts = local_part(q + 1)
@@ -303,10 +307,12 @@
         for k in range(1, devices):
             stage_copy(n, prompt, layer, lax.rem(me + k, devices)).start()
 
-        for j in range(tiles):
-            for k in range(3):
-                row = k * 2 * 16 + j
-                tail_f_ref[pl.ds(layer * 16 + row, 1), :] = u_ref[j, seg + HALO - 3 + k:seg + HALO - 2 + k, :]
+        for l in range(2):
+            @pl.when(layer == l)
+            def _():
+                for j in range(tiles):
+                    for k in range(3):
+                        tail_f_ref[k, l:l + 1, j * LANES:(j + 1) * LANES] = u_ref[j, seg + HALO - 3 + k:seg + HALO - 2 + k, :]
 
         @pl.when(layer == 1)
         def _():
@@ -346,7 +352,8 @@
                 stage_local(n, batch - 1, n).wait()
                 for k in range(1, devices):
                     stage_copy(n, batch - 1, n, lax.rem(me + k, devices)).wait_send()
-            for group in range(tail_send.shape[0]):
+            @pl.loop(0, tail_send.shape[0])
+            def _(group):
                 tail_local(group).wait()
                 for k in range(1, devices):
                     tail_copy(group, lax.rem(me + k, devices)).wait_send()
@@ -377,7 +384,7 @@
             grid=(batch, layers),
             out_shape=(jax.ShapeDtypeStruct((batch, seg, d_model), jnp.float32),
                        jax.ShapeDtypeStruct((batch, layers, per_device, d_state), jnp.float32),
-                       jax.ShapeDtypeStruct((batch, 6 * 16, LANES), jnp.bfloat16)),
+                       jax.ShapeDtypeStruct((batch, 3, layers, conv_dim), jnp.bfloat16)),
             in_specs=[block, hbm, hbm] + [whole(a) for a in params],
             out_specs=(block, hbm, hbm),
             scratch_shapes=[pltpu.VMEM((seg, d_model), jnp.float32),
@@ -388,27 +395,26 @@
                             pltpu.VMEM((tiles, HALO + seg, LANES), jnp.float32),
                             pltpu.VMEM((SLOTS, d_state, d_inner), jnp.float32),
                             pltpu.VMEM((SLOTS, d_state, d_inner), jnp.float32),
-                            pltpu.VMEM((SLOTS, 4, 16, LANES), jnp.bfloat16),
-                            pltpu.VMEM((SLOTS, 4, 16, LANES), jnp.bfloat16),
-                            pltpu.VMEM((2, 4, 16, LANES), jnp.float32),
+                            pltpu.VMEM((SLOTS, 48, LANES), jnp.bfloat16),
+                            pltpu.VMEM((SLOTS, 48, LANES), jnp.bfloat16),
+                            pltpu.VMEM((2, 48, LANES), jnp.float32),
                             pltpu.VMEM((seg, d_inner), jnp.float32),
                             pltpu.VMEM((2, seg_count, per_device, d_state), jnp.float32),
-                            pltpu.VMEM((6 * 16, LANES), jnp.float32),
-                            pltpu.VMEM((batch, 6 * 16, LANES), jnp.bfloat16),
+                            pltpu.VMEM((3, layers, conv_dim), jnp.float32),
+                            pltpu.VMEM((batch, 3, layers, conv_dim), jnp.bfloat16),
                             pltpu.SemaphoreType.DMA((layers,)),
                             pltpu.SemaphoreType.DMA((2,)),
                             pltpu.SemaphoreType.DMA((SLOTS, quads)),
                             pltpu.SemaphoreType.DMA((SLOTS, quads)),
-                            pltpu.SemaphoreType.DMA((SLOTS, 4)),
-                            pltpu.SemaphoreType.DMA((SLOTS, 4)),
+                            pltpu.SemaphoreType.DMA((SLOTS, 2)),
+                            pltpu.SemaphoreType.DMA((SLOTS, 2)),
                             pltpu.SemaphoreType.DMA((2, seg_count)),
                             pltpu.SemaphoreType.DMA,
-                            pltpu.SemaphoreType.DMA((8, seg_count)),
+                            pltpu.SemaphoreType.DMA((batch, seg_count)),
                             pltpu.SemaphoreType.DMA,
                             pltpu.SemaphoreType.REGULAR],
             compiler_params=pltpu.CompilerParams(dimension_semantics=('arbitrary',) * 2, vmem_limit_bytes=67043328, collective_id=0, has_side_effects=True),
         )(resid, jnp.swapaxes(w_in, 1, 2), w_out, *params)
-        tails = tail.reshape(batch, 3, layers, 16, LANES)[:, :, :, :tiles].reshape(batch, 3, layers, conv_dim)
-        return out, state.reshape(batch, layers, heads // seg_count, head_dim, d_state), jnp.transpose(tails, (0, 2, 3, 1))
+        return out, state.reshape(batch, layers, heads // seg_count, head_dim, d_state), jnp.transpose(tail, (0, 2, 3, 1))
 
     return jax.shard_map(forward, mesh=mesh, in_specs=(P('dp', 'sp', None), P(), P(), P(), P(), P(), P(), P(), P(), P()), out_specs=(P('dp', 'sp', None), P('dp', None, 'sp', None, None), P('dp', None, None, None)), check_vma=False)

time: 610 us -> 606 us (level)
  no operation moved by 1% of the time
where the time goes in v6:
time: 606 us
  Pallas kernels  584 us (96%)
  local copies, waits for them, and re-layouts  21.4 us (4%)
    pallas_call x1, Pallas kernels, forward(): pl.pallas_call(functools.partial(forward_kernel, (d_inner, heads, seg, se...  584 us
    unnamed x7, local copies, waits for them, and re-layouts  21.4 us

profile of v6, /device:TPU:0, one launch (start us, length us, event | category | flops | bytes accessed | tf_op | source)
XLA Modules:
  0.0 606.3 jit_solution(11261942088016684903)
XLA Ops:
  0.6 584.2 %shard_map.121 = (f32[32,256,768]{2,1,0:T(8,128)}, f32[32,2,192,128]{3,2,1,0:T(8,128)}, bf16[32,3,2,1792]{3,2,1,0:T(2,128)(2,1)}) custom-call(f32[32,256,768]{2,1,0:T(8,128)} %x_ref.1, bf16[2,3352,768]{2,1,0:T(8,128)(2,1)} %bitcast.4, bf16[2,1536,768]{2,1,0:T(8,128)(2,1)} %w_out_hbm.1, f32[2,768]{1,0:T(2,128)} %pre_ref.1, f32[2,4,1792]{2,1,0:T(4,128)} %bitcast.7, ...), custom_call_target="tpu_custom_call" | custom-call | tf_op jit(solution)/shard_map/pallas_call | solution.py:382
  584.8 0.0 copy-start
  584.9 17.8 %copy.16 = f32[32,256,768]{2,1,0:T(8,128)} copy(f32[32,256,768]{2,1,0:T(8,128)} %get-tuple-element.12) | data formatting | bytes 50331648
  602.6 0.1 copy-done
  602.7 0.0 copy-start.1
  602.7 2.7 copy.17
  605.4 0.0 copy-done.1
  605.4 0.8 copy.18
Async XLA Ops:
  584.8 17.9 %copy-start = (f32[32,2,192,128]{3,2,1,0:T(8,128)S(1)}, f32[32,2,192,128]{3,2,1,0:T(8,128)}, u32[]{:S(2)}) copy-start(f32[32,2,192,128]{3,2,1,0:T(8,128)} %get-tuple-element.7) | copy-start | bytes 18874372
  602.7 2.7 copy-start.1

commit v7 on v6

--- a/solution.py
+++ b/solution.py
@@ -96,9 +96,8 @@
 
     @pl.when(step == 0)
     def _():
-        for l in range(2):
-            w_in_copy(l).start()
-            w_out_copy(l).start()
+        w_in_copy(0).start()
+        w_out_copy(0).start()
         barrier = pltpu.get_barrier_semaphore()
         for k in range(1, devices):
             pl.semaphore_signal(barrier, inc=1, device_id={'sp': lax.rem(me + k, devices)}, device_id_type=pl.DeviceIdType.MESH)
@@ -131,6 +130,12 @@
     def _():
         w_in_copy(layer).wait()
         w_out_copy(layer).wait()
+
+        @pl.when(layer == 0)
+        def _():
+            w_in_copy(1).start()
+            w_out_copy(1).start()
+
         w_in_ref[layer, w_in_hbm.shape[1]:, :] = jnp.zeros((w_in_ref.shape[1] - w_in_hbm.shape[1], w_in_ref.shape[2]), jnp.bfloat16)
 
     @pl.when((me < last_device) & (step >= slots))

time: 606 us -> 606 us (level)
  no operation moved by 1% of the time
where the time goes in v7:
time: 606 us
  Pallas kernels  584 us (96%)
  local copies, waits for them, and re-layouts  21.4 us (4%)
    pallas_call x1, Pallas kernels, forward(): pl.pallas_call(functools.partial(forward_kernel, (d_inner, heads, seg, se...  584 us
    unnamed x7, local copies, waits for them, and re-layouts  21.4 us

profile of v7, /device:TPU:0, one launch (start us, length us, event | category | flops | bytes accessed | tf_op | source)
XLA Modules:
  0.0 606.3 jit_solution(4123575449186627975)
XLA Ops:
  0.6 584.2 %shard_map.121 = (f32[32,256,768]{2,1,0:T(8,128)}, f32[32,2,192,128]{3,2,1,0:T(8,128)}, bf16[32,3,2,1792]{3,2,1,0:T(2,128)(2,1)}) custom-call(f32[32,256,768]{2,1,0:T(8,128)} %x_ref.1, bf16[2,3352,768]{2,1,0:T(8,128)(2,1)} %bitcast.4, bf16[2,1536,768]{2,1,0:T(8,128)(2,1)} %w_out_hbm.1, f32[2,768]{1,0:T(2,128)} %pre_ref.1, f32[2,4,1792]{2,1,0:T(4,128)} %bitcast.7, ...), custom_call_target="tpu_custom_call" | custom-call | tf_op jit(solution)/shard_map/pallas_call | solution.py:387
  584.8 0.0 copy-start
  584.9 17.8 %copy.16 = f32[32,256,768]{2,1,0:T(8,128)} copy(f32[32,256,768]{2,1,0:T(8,128)} %get-tuple-element.12) | data formatting | bytes 50331648
  602.6 0.1 copy-done
  602.7 0.0 copy-start.1
  602.7 2.7 copy.17
  605.4 0.0 copy-done.1
  605.4 0.8 copy.18
Async XLA Ops:
  584.8 17.9 %copy-start = (f32[32,2,192,128]{3,2,1,0:T(8,128)S(1)}, f32[32,2,192,128]{3,2,1,0:T(8,128)}, u32[]{:S(2)}) copy-start(f32[32,2,192,128]{3,2,1,0:T(8,128)} %get-tuple-element.7) | copy-start | bytes 18874372
  602.7 2.7 copy-start.1
